TPU v7x, 32 devices: a whole 2x2x4 slice. The times are simulated.
32 devices in a mesh: dp: 8 (over y, x, core), mp: 4 (over z).
Axes of the slice: x: 2, y: 2, z: 4, core: 2. Of those that a mesh axis runs over, the one named last changes fastest.
Arguments:
- inputs: bfloat16 [8192, 2048], P(('dp', 'mp')), may hold values from -6 to 6
- segments: int32 [8, 1024], P('dp'), may hold values from 0 to 5, never falling along the last dimension, each value on 1 to 512 neighbouring positions
- first_norm_gain: float32 [2048], replicated, may hold values from 0.1 to 1.9
- w_query: bfloat16 [2048, 2048], P('dp', 'mp'), may hold values from -0.125 to 0.125
- w_key: bfloat16 [2048, 2048], P('dp', 'mp'), may hold values from -0.125 to 0.125
- w_value: bfloat16 [2048, 3456], P('dp', 'mp'), may hold values from -0.125 to 0.125
- w_gate: bfloat16 [2048, 3456], P('dp', 'mp'), may hold values from -0.125 to 0.125
- w_out: bfloat16 [3456, 2048], P('mp', 'dp'), may hold values from -0.21875 to 0.21875
- second_norm_gain: float32 [2048], replicated, may hold values from 0.1 to 1.9
- w_glu_gate: bfloat16 [2048, 3456], P('dp', 'mp'), may hold values from -0.125 to 0.125
- w_glu_up: bfloat16 [2048, 3456], P('dp', 'mp'), may hold values from -0.125 to 0.125
- w_down: bfloat16 [3456, 2048], P('mp', 'dp'), may hold values from -0.21875 to 0.21875
- cotangent: bfloat16 [8192, 2048], P(('dp', 'mp')), may hold values from -9 to 9
Outputs:
- outputs: bfloat16 [8192, 2048], P(('dp', 'mp'))
- input_gradient: float32 [8192, 2048], P(('dp', 'mp'))
- grad_norm1_gain: float32 [2048], replicated
- grad_w_query: float32 [2048, 2048], P('dp', 'mp')
- grad_w_key: float32 [2048, 2048], P('dp', 'mp')
- grad_w_value: float32 [2048, 3456], P('dp', 'mp')
- grad_w_gate: float32 [2048, 3456], P('dp', 'mp')
- grad_w_out: float32 [3456, 2048], P('mp', 'dp')
- grad_norm2_gain: float32 [2048], replicated
- grad_w_glu_gate: float32 [2048, 3456], P('dp', 'mp')
- grad_w_glu_up: float32 [2048, 3456], P('dp', 'mp')
- grad_w_down: float32 [3456, 2048], P('mp', 'dp')
Inputs may be any that keep to these rules, and one draw needn't show every extreme that they name: `segments`: within a sequence the document numbers never fall; each document holds 1 to 512 tokens and one holds exactly 512.
All inputs are finite; a program needn't handle non-finite values.
Results may differ from a plain program's by a relative error of at most 0.024.
Values may be sent and summed in bfloat16 or wider, within the bound.
A program may use at most 256 MiB of HBM per device.

v0:
```python
import jax
import jax.numpy as jnp
from jax import lax
from jax.sharding import PartitionSpec as P

H = 8
HK = 256
HV = 432
LEN = 1024
CHUNKS = 2
epsilon = 1e-05
group_epsilon = 1.0
BF = jnp.bfloat16
F32 = jnp.float32


def layer_norm(values_in, offset):
    centre = jnp.mean(values_in, axis=-1, keepdims=True)
    centred = values_in - centre
    variance = jnp.mean(centred * centred, axis=-1, keepdims=True)
    scaling = lax.rsqrt(variance + offset)
    return (centred * scaling, scaling)


def norm_back(grad_hat, normed_hat, scaling):
    first_mean = jnp.mean(grad_hat, axis=-1, keepdims=True)
    second_mean = jnp.mean(grad_hat * normed_hat, axis=-1, keepdims=True)
    return scaling * (grad_hat - first_mean - normed_hat * second_mean)


def glu_act(gate_pre, up_pre):
    return jax.nn.gelu(gate_pre, approximate=True) * up_pre


def dot_nt(a, b):
    return lax.dot_general(a, b, (((1,), (1,)), ((), ())), preferred_element_type=F32)


def dot_nn(a, b):
    return lax.dot_general(a, b, (((1,), (0,)), ((), ())), preferred_element_type=F32)


def dot_tn(a, b):
    return lax.dot_general(a, b, (((0,), (0,)), ((), ())), preferred_element_type=F32)


def line_gather(own, n, place):
    right, left = ([None], [None])
    r = l = own
    for step in range(1, n):
        r = lax.ppermute(r, "mp", [(i, i + 1) for i in range(step - 1, n - 1)])
        l = lax.ppermute(l, "mp", [(i, i - 1) for i in range(1, n - step + 1)])
        right.append(r)
        left.append(l)
    return [own] + [jnp.where(place >= k, right[k], left[n - k]) for k in range(1, n)]


def line_scatter(slots, n):
    r = l = None
    for step in range(1, n):
        send_r, send_l = (slots[step], slots[n - step])
        if r is not None:
            send_r = (send_r.astype(F32) + r.astype(F32)).astype(BF)
            send_l = (send_l.astype(F32) + l.astype(F32)).astype(BF)
        r = lax.ppermute(send_r, "mp", [(i, i + 1) for i in range(step)])
        l = lax.ppermute(send_l, "mp", [(i, i - 1) for i in range(n - step, n)])
    return slots[0].astype(F32) + r.astype(F32) + l.astype(F32)


def body(
    inputs,
    segments,
    first_norm_gain,
    w_query,
    w_key,
    w_value,
    w_gate,
    w_out,
    second_norm_gain,
    w_glu_gate,
    w_glu_up,
    w_down,
    cotangent,
):
    n = lax.axis_size("mp")
    place = lax.axis_index("mp")
    heads = H // n
    head_start = place * heads
    rows, width = inputs.shape
    piece = rows // CHUNKS
    per = n * piece
    nk, nv, nf = (heads * HK, heads * HV, w_down.shape[0])
    pack_one = jnp.concatenate([w_query.T, w_key.T, w_value.T, w_gate.T], axis=0)
    weight_one = lax.all_gather(pack_one, "dp", axis=1, tiled=True)
    out_weight = lax.all_gather(w_out, "dp", axis=1, tiled=True)
    pack_two = jnp.concatenate([w_glu_gate.T, w_glu_up.T, w_down], axis=0)
    weight_two = lax.all_gather(pack_two, "dp", axis=1, tiled=True)
    glu_weight, down_weight = (weight_two[: 2 * nf], weight_two[2 * nf :])

    def cut(array):
        return [array[h * piece : (h + 1) * piece] for h in range(CHUNKS)]

    def gather(block):
        return jnp.concatenate(line_gather(block, n, place), axis=0)

    def scatter(part):
        return line_scatter([part[k * piece : (k + 1) * piece] for k in range(n)], n)

    inputs_cut = [c.astype(F32) for c in cut(inputs)]
    first_hat, first_scale, first_rows = ([], [], [])
    for x in inputs_cut:
        hat, scale = layer_norm(x, epsilon)
        first_hat.append(hat)
        first_scale.append(scale)
        first_rows.append((hat * first_norm_gain).astype(BF))
    rows_one = jnp.concatenate([gather(block) for block in first_rows], axis=0)
    tokens = rows_one.shape[0]
    slot_shard = lax.rem(place - jnp.arange(n) + n, n)
    places = (
        slot_shard[None, :, None] * rows
        + jnp.arange(CHUNKS)[:, None, None] * piece
        + jnp.arange(piece)[None, None, :]
    ).reshape(tokens)
    seg = segments.reshape(n, CHUNKS, piece)[::-1]
    seg = lax.dynamic_slice_in_dim(jnp.concatenate([seg, seg], axis=0), n - 1 - place, n, axis=0)
    seg = seg.transpose(1, 0, 2).reshape(tokens)
    query_key = dot_nt(rows_one, weight_one[: 2 * nk]).astype(BF)
    value = dot_nt(rows_one, weight_one[2 * nk : 2 * nk + nv]).astype(BF)
    gate_pre = dot_nt(rows_one, weight_one[2 * nk + nv :])
    query = query_key[:, :nk].reshape(tokens, heads, HK)
    key = query_key[:, nk:].reshape(tokens, heads, HK)
    value = value.reshape(tokens, heads, HV)
    distance = places[:, None] - places[None, :]
    allowed = (distance >= 0) & (seg[:, None] == seg[None, :])
    log_gamma = jnp.log1p(-jnp.exp2(-5.0 - (head_start + jnp.arange(heads)).astype(F32)))
    exponent = jnp.where(allowed[None], distance[None].astype(F32) * log_gamma[:, None, None], 0.0)
    mask = jnp.where(allowed[None], jnp.exp(exponent), 0.0) * HK ** (-0.5)
    scores = (jnp.einsum("thk,shk->hts", query, key, preferred_element_type=F32) * mask).astype(BF)
    retained = jnp.einsum("hts,shv->thv", scores, value, preferred_element_type=F32)
    normalized, scale_group = layer_norm(retained, group_epsilon)
    normal_flat = normalized.reshape(tokens, nv)
    swish = jax.nn.silu(gate_pre)
    gated = (swish * normal_flat).astype(BF)
    cot_cut = cut(cotangent)
    cot_rows = [gather(c) for c in cot_cut]

    def group(array, h):
        return array[h * per : (h + 1) * per]

    outputs, second_gain, middle_grad = ([], [], [])
    rows_two, hidden_all, d_glu_all, mid_rows = ([], [], [], [])
    for h in range(CHUNKS):
        attn_part = dot_nn(group(gated, h), out_weight).astype(BF)
        middle = inputs_cut[h] + scatter(attn_part)
        hat, scale = layer_norm(middle, epsilon)
        rows_h = gather((hat * second_norm_gain).astype(BF))
        rows_two.append(rows_h)
        glu = dot_nt(rows_h, glu_weight)
        glu_gate, glu_up = (glu[:, :nf], glu[:, nf:])
        d_hidden = dot_nt(cot_rows[h], down_weight)
        hidden, pullback = jax.vjp(glu_act, glu_gate, glu_up)
        hidden = hidden.astype(BF)
        d_glu = jnp.concatenate([d.astype(BF) for d in pullback(d_hidden)], axis=1)
        hidden_all.append(hidden)
        d_glu_all.append(d_glu)
        second_grad = scatter(dot_nn(d_glu, glu_weight).astype(BF))
        second_gain.append(jnp.sum(hat * second_grad, axis=0))
        grad_h = cot_cut[h].astype(F32) + norm_back(second_grad * second_norm_gain, hat, scale)
        middle_grad.append(grad_h)
        mid_rows.append(gather(grad_h.astype(BF)))
        outputs.append(middle + scatter(dot_nn(hidden, down_weight).astype(BF)))
    cot_all = jnp.concatenate(cot_rows, axis=0)
    grads_two = jnp.concatenate(
        [
            dot_tn(jnp.concatenate(d_glu_all, axis=0), jnp.concatenate(rows_two, axis=0)),
            dot_tn(jnp.concatenate(hidden_all, axis=0), cot_all),
        ],
        axis=0,
    ).astype(BF)
    summed_two = lax.psum_scatter(grads_two, "dp", scatter_dimension=1, tiled=True).astype(F32)
    mid_all = jnp.concatenate(mid_rows, axis=0)
    d_gated = dot_nt(mid_all, out_weight)
    sigmoid_gate = jax.nn.sigmoid(gate_pre)
    d_gate_pre = (
        d_gated * normal_flat * (sigmoid_gate + gate_pre * sigmoid_gate * (1.0 - sigmoid_gate))
    ).astype(BF)
    d_normalized = (d_gated * swish).reshape(tokens, heads, HV)
    d_retained = norm_back(d_normalized, normalized, scale_group).astype(BF)
    grads_out = jnp.concatenate(
        [dot_tn(gated, mid_all).astype(BF), dot_tn(d_gate_pre, rows_one).astype(BF)], axis=0
    )
    summed_out = lax.psum_scatter(grads_out, "dp", scatter_dimension=1, tiled=True).astype(F32)
    d_value = jnp.einsum("hts,thv->shv", scores, d_retained, preferred_element_type=F32).astype(BF)
    d_scores = (
        jnp.einsum("thv,shv->hts", d_retained, value, preferred_element_type=F32) * mask
    ).astype(BF)
    d_query = jnp.einsum("hts,shk->thk", d_scores, key, preferred_element_type=F32).astype(BF)
    d_key = jnp.einsum("hts,thk->shk", d_scores, query, preferred_element_type=F32).astype(BF)
    d_qkv = jnp.concatenate(
        [d_query.reshape(tokens, nk), d_key.reshape(tokens, nk), d_value.reshape(tokens, nv)],
        axis=1,
    )
    grads_one = dot_tn(d_qkv, rows_one).astype(BF)
    summed_one = lax.psum_scatter(grads_one, "dp", scatter_dimension=1, tiled=True).astype(F32)
    d_one = jnp.concatenate([d_qkv, d_gate_pre], axis=1)
    input_gradient, first_gain = ([], [])
    for h in range(CHUNKS):
        first_grad = scatter(dot_nn(group(d_one, h), weight_one).astype(BF))
        first_gain.append(jnp.sum(first_hat[h] * first_grad, axis=0))
        input_gradient.append(
            middle_grad[h] + norm_back(first_grad * first_norm_gain, first_hat[h], first_scale[h])
        )
    gains = lax.psum(jnp.stack([sum(first_gain), sum(second_gain)]), ("dp", "mp"))
    return (
        jnp.concatenate(outputs, axis=0).astype(BF),
        jnp.concatenate(input_gradient, axis=0),
        gains[0],
        summed_one[:nk].T,
        summed_one[nk : 2 * nk].T,
        summed_one[2 * nk :].T,
        summed_out[nv:].T,
        summed_out[:nv],
        gains[1],
        summed_two[:nf].T,
        summed_two[nf : 2 * nf].T,
        summed_two[2 * nf :],
    )


def solution(mesh):
    split = P(("dp", "mp"), None)
    wide, tall = (P("dp", "mp"), P("mp", "dp"))
    return jax.shard_map(
        body,
        mesh=mesh,
        in_specs=(
            split,
            P("dp", None),
            P(),
            wide,
            wide,
            wide,
            wide,
            tall,
            P(),
            wide,
            wide,
            tall,
            split,
        ),
        out_specs=(split, split, P(), wide, wide, wide, wide, tall, P(), wide, wide, tall),
        check_vma=False,
    )
```

profile of v0, /device:TPU:0, one launch (start us, length us, event | category | flops | bytes accessed | tf_op | source)
XLA Modules:
  0.0 846.9 jit_solution(8839183228155669539)
XLA Ops:
  15.7 5.6 collective-permute-start
  21.3 10.0 %collective-permute-done.1 = bf16[128,2048]{1,0:T(8,128)(2,1)S(1)} collective-permute-done((bf16[128,2048]{1,0:T(8,128)(2,1)S(1)}, bf16[128,2048]{1,0:T(8,128)(2,1)S(1)}, u32[]{:S(2)}, u32[]{:S(2)}) %collective-permute-start.1) | collective-permute-done | bytes 524320 | tf_op jit(solution)/shard_map/ppermute | solution.py:52
  33.3 13.1 %collective-permute-done.2 = bf16[128,2048]{1,0:T(8,128)(2,1)S(1)} collective-permute-done((bf16[128,2048]{1,0:T(8,128)(2,1)S(1)}, bf16[128,2048]{1,0:T(8,128)(2,1)S(1)}, u32[]{:S(2)}, u32[]{:S(2)}) %collective-permute-start.2) | collective-permute-done | bytes 524320 | tf_op jit(solution)/shard_map/ppermute | solution.py:52
  48.6 12.1 %collective-permute-done.3 = bf16[128,2048]{1,0:T(8,128)(2,1)} collective-permute-done((bf16[128,2048]{1,0:T(8,128)(2,1)S(1)}, bf16[128,2048]{1,0:T(8,128)(2,1)}, u32[]{:S(2)}, u32[]{:S(2)}) %collective-permute-start.3) | collective-permute-done | bytes 524320 | tf_op jit(solution)/shard_map/ppermute | solution.py:52
  73.0 6.1 collective-permute-done.7
  83.5 8.2 collective-permute-done.8
  95.1 8.5 %collective-permute-done.9 = bf16[128,2048]{1,0:T(8,128)(2,1)} collective-permute-done((bf16[128,2048]{1,0:T(8,128)(2,1)S(1)}, bf16[128,2048]{1,0:T(8,128)(2,1)}, u32[]{:S(2)}, u32[]{:S(2)}) %collective-permute-start.9) | collective-permute-done | bytes 524320 | tf_op jit(solution)/shard_map/ppermute | solution.py:52
  107.4 8.1 fusion.74
  132.7 6.0 fusion.27
  150.5 6.6 collective-permute-done.30
  162.6 5.8 collective-permute-done.12
  197.0 8.1 collective-permute-start.48
  206.4 6.9 collective-permute-done.14
  221.1 17.0 %collective-permute-start.18 = (bf16[128,2048]{1,0:T(8,128)(2,1)S(1)}, bf16[128,2048]{1,0:T(8,128)(2,1)S(1)}, u32[]{:S(2)}, u32[]{:S(2)}) collective-permute-start(bf16[128,2048]{1,0:T(8,128)(2,1)S(1)} %get-tuple-element.72), channel_id=1, source_target_pairs={{0,1},{1,2},{2,3},{4,5},{5,6},{6,7},{8,9},{9,10},{10,11},{12,13},{... | collective-permute-start | bytes 1572872 | tf_op jit(solution)/shard_map/ppermute | solution.py:51
  240.2 8.6 %collective-permute-done.51 = bf16[128,2048]{1,0:T(8,128)(2,1)S(1)} collective-permute-done((bf16[128,2048]{1,0:T(8,128)(2,1)S(1)}, bf16[128,2048]{1,0:T(8,128)(2,1)S(1)}, u32[]{:S(2)}, u32[]{:S(2)}) %collective-permute-start.51) | collective-permute-done | bytes 524320 | tf_op jit(solution)/shard_map/ppermute | solution.py:52
  259.9 7.3 collective-permute-done.21
  270.7 7.8 fusion.6
  293.0 7.0 collective-permute-done.54
  309.0 16.9 %collective-permute-start.25 = (bf16[128,2048]{1,0:T(8,128)(2,1)S(1)}, bf16[128,2048]{1,0:T(8,128)(2,1)S(1)}, u32[]{:S(2)}, u32[]{:S(2)}) collective-permute-start(bf16[128,2048]{1,0:T(8,128)(2,1)S(1)} %get-tuple-element.135), channel_id=1, source_target_pairs={{0,1},{1,2},{4,5},{5,6},{8,9},{9,10},{12,13},{13,14},{16,17},{17,1... | collective-permute-start | bytes 1572872 | tf_op jit(solution)/shard_map/ppermute | solution.py:65
  327.3 12.0 %collective-permute-start.56 = (bf16[128,2048]{1,0:T(8,128)(2,1)S(1)}, bf16[128,2048]{1,0:T(8,128)(2,1)S(1)}, u32[]{:S(2)}, u32[]{:S(2)}) collective-permute-start(bf16[128,2048]{1,0:T(8,128)(2,1)S(1)} %get-tuple-element.127), channel_id=1, source_target_pairs={{0,1},{1,2},{2,3},{4,5},{5,6},{6,7},{8,9},{9,10},{10,11},{12,13},{... | collective-permute-start | bytes 1572872 | tf_op jit(solution)/shard_map/ppermute | solution.py:65
  341.1 10.1 %collective-permute-start.26 = (bf16[128,2048]{1,0:T(8,128)(2,1)S(1)}, bf16[128,2048]{1,0:T(8,128)(2,1)S(1)}, u32[]{:S(2)}, u32[]{:S(2)}) collective-permute-start(bf16[128,2048]{1,0:T(8,128)(2,1)S(1)} %get-tuple-element.133), channel_id=1, source_target_pairs={{0,1},{1,2},{2,3},{4,5},{5,6},{6,7},{8,9},{9,10},{10,11},{12,13},{... | collective-permute-start | bytes 1572872 | tf_op jit(solution)/shard_map/ppermute | solution.py:65
  357.8 12.8 %collective-permute-done.29 = bf16[128,2048]{1,0:T(8,128)(2,1)S(1)} collective-permute-done((bf16[128,2048]{1,0:T(8,128)(2,1)S(1)}, bf16[128,2048]{1,0:T(8,128)(2,1)S(1)}, u32[]{:S(2)}, u32[]{:S(2)}) %collective-permute-start.29) | collective-permute-done | bytes 524320 | tf_op jit(solution)/shard_map/ppermute | solution.py:66
  392.8 9.9 %collective-permute-done.61 = bf16[128,2048]{1,0:T(8,128)(2,1)S(1)} collective-permute-done((bf16[128,2048]{1,0:T(8,128)(2,1)S(1)}, bf16[128,2048]{1,0:T(8,128)(2,1)S(1)}, u32[]{:S(2)}, u32[]{:S(2)}) %collective-permute-start.61) | collective-permute-done | bytes 524320 | tf_op jit(solution)/shard_map/ppermute | solution.py:52
  405.5 8.5 %collective-permute-done.37 = bf16[128,2048]{1,0:T(8,128)(2,1)S(1)} collective-permute-done((bf16[128,2048]{1,0:T(8,128)(2,1)S(1)}, bf16[128,2048]{1,0:T(8,128)(2,1)S(1)}, u32[]{:S(2)}, u32[]{:S(2)}) %collective-permute-start.37) | collective-permute-done | bytes 524320 | tf_op jit(solution)/shard_map/ppermute | solution.py:52
  416.0 9.2 %collective-permute-done.68 = bf16[128,2048]{1,0:T(8,128)(2,1)S(1)} collective-permute-done((bf16[128,2048]{1,0:T(8,128)(2,1)S(1)}, bf16[128,2048]{1,0:T(8,128)(2,1)S(1)}, u32[]{:S(2)}, u32[]{:S(2)}) %collective-permute-start.68) | collective-permute-done | bytes 524320 | tf_op jit(solution)/shard_map/ppermute | solution.py:52
  428.6 7.7 collective-permute-done.38
  444.4 8.7 %collective-permute-done.39 = bf16[128,2048]{1,0:T(8,128)(2,1)S(1)} collective-permute-done((bf16[128,2048]{1,0:T(8,128)(2,1)S(1)}, bf16[128,2048]{1,0:T(8,128)(2,1)S(1)}, u32[]{:S(2)}, u32[]{:S(2)}) %collective-permute-start.39) | collective-permute-done | bytes 524320 | tf_op jit(solution)/shard_map/ppermute | solution.py:52
  456.8 7.2 fusion.4
  477.0 7.2 fusion.34
  494.4 5.4 collective-permute-done.72
  529.2 6.3 collective-permute-done.74
  535.5 6.1 collective-permute-done.77
  546.8 7.6 collective-permute-start.78
  554.4 6.6 collective-permute-done.79
  563.0 9.1 %collective-permute-done.80 = bf16[128,2048]{1,0:T(8,128)(2,1)S(1)} collective-permute-done((bf16[128,2048]{1,0:T(8,128)(2,1)S(1)}, bf16[128,2048]{1,0:T(8,128)(2,1)S(1)}, u32[]{:S(2)}, u32[]{:S(2)}) %collective-permute-start.80) | collective-permute-done | bytes 524320 | tf_op jit(solution)/shard_map/ppermute | solution.py:52
  574.1 9.1 %collective-permute-done.81 = bf16[128,2048]{1,0:T(8,128)(2,1)S(1)} collective-permute-done((bf16[128,2048]{1,0:T(8,128)(2,1)S(1)}, bf16[128,2048]{1,0:T(8,128)(2,1)S(1)}, u32[]{:S(2)}, u32[]{:S(2)}) %collective-permute-start.81) | collective-permute-done | bytes 524320 | tf_op jit(solution)/shard_map/ppermute | solution.py:52
  588.9 6.6 fusion.159
  602.1 7.3 pad_maximum_fusion.1
  628.1 13.3 %convolution_convert_fusion.1 = bf16[1888,2048]{1,0:T(8,128)(2,1)} fusion(bf16[1024,2048]{1,0:T(8,128)(2,1)S(1)} %copy-done.50, bf16[1024,864]{0,1:T(8,128)(2,1)S(1)} %bitcast.92, bf16[1024,512]{0,1:T(8,128)(2,1)S(1)} %bitcast.100, bf16[1024,512]{0,1:T(8,128)(2,1)S(1)} %bitcast.102), kind=kOutput, calls=%fused_computation.5 | convolution fusion | flops 7934312448 | bytes 15794176 | tf_op jit(solution)/shard_map/dot_general | solution.py:44
  641.8 6.7 convolution_convert_fusion.2
  648.5 21.0 %convolution_convert_fusion = bf16[1728,2048]{1,0:T(8,128)(2,1)S(1)} fusion(bf16[1024,2048]{1,0:T(8,128)(2,1)} %get-tuple-element.57, bf16[512,864]{0,1:T(8,128)(2,1)S(1)} %copy-done.88, bf16[512,864]{0,1:T(8,128)(2,1)S(1)} %copy-done.86, bf16[512,864]{0,1:T(8,128)(2,1)S(1)} %copy-done.84, bf16[512,864]{0,1:T(8,128)(2,1)S(1)} %copy-done.82), kind=kOutput, calls=%fused_computation.4 | convolution fusion | flops 7265452032 | bytes 14811136 | tf_op jit(solution)/shard_map/dot_general | solution.py:44
  669.5 12.8 %pad_maximum_fusion = bf16[2592,2048]{1,0:T(8,128)(2,1)} fusion(bf16[864,2048]{1,0:T(8,128)(2,1)S(1)} %convolution_convert_fusion.2, bf16[1728,2048]{1,0:T(8,128)(2,1)S(1)} %convolution_convert_fusion), kind=kLoop, calls=%fused_computation | loop fusion | flops 21233664 | bytes 21233664 | tf_op jit(solution)/shard_map/concatenate | solution.py:173
  688.1 10.2 %convolution_convert_fusion.6 = bf16[512,2048]{1,0:T(8,128)(2,1)S(1)} fusion(bf16[2752,2048]{1,0:T(8,128)(2,1)} %all-gather.4.cloned.1.call-done, bf16[1024,2752]{0,1:T(8,128)(2,1)S(1)} %pad_maximum_fusion.2), kind=kOutput, calls=%fused_computation.55 | convolution fusion | flops 5772410880 | bytes 16187392 | tf_op jit(solution)/shard_map/dot_general | solution.py:40
  700.5 6.6 convolution_convert_fusion.5
  717.4 5.8 collective-permute-done.90
  740.9 7.9 collective-permute-start.92
  761.2 40.4 %psum.7 = f32[2,2048]{1,0:T(2,128)S(1)} all-reduce(f32[2,2048]{1,0:T(2,128)S(1)} %pad_maximum_fusion.7), channel_id=1, replica_groups=mesh['dp'=8,'mp'=4] {'dp','mp'}, use_global_device_ids=true, to_apply=%region_24.25 | all-reduce | flops 4096 | bytes 32768 | tf_op jit(solution)/shard_map/psum | solution.py:213
  815.8 19.9 %reduce-scatter.8.cloned.1.call-done = bf16[2592,256]{1,0:T(8,128)(2,1)} async-done(((bf16[2592,2048]{1,0:T(8,128)(2,1)}), bf16[2592,256]{1,0:T(8,128)(2,1)}) %reduce-scatter.8.cloned.1.call-update) | async-done | bytes 1327120 | tf_op jit(solution)/shard_map/reduce_scatter | solution.py:180
  (503 shorter events, 357.8 us)
Async XLA Ops:
  7.2 100.2 %all-gather.4.cloned.1.call-start = ((), (), s32[]{:S(2)}) async-start(), calls=%async_computation.3 | async-start | bytes 12681216 | tf_op jit(solution)/shard_map/all_gather | solution.py:94
  11.9 126.8 %all-gather.6.cloned.1.call-start = ((), (), s32[]{:S(2)}) async-start(), calls=%async_computation.4 | async-start | bytes 3981312 | tf_op jit(solution)/shard_map/all_gather | solution.py:95
  12.6 258.0 %all-gather.8.cloned.1.call-start = ((), (), s32[]{:S(2)}) async-start(), calls=%async_computation.5 | async-start | bytes 11943936 | tf_op jit(solution)/shard_map/all_gather | solution.py:97
  68.2 738.9 %reduce-scatter.6.cloned.1.call-start = ((), (), s32[]{:S(2)}) async-start(), calls=%async_computation.7 | async-start | bytes 7962624 | tf_op jit(solution)/shard_map/reduce_scatter | solution.py:192
  148.4 20.0 %collective-permute-start.12 = (bf16[128,2048]{1,0:T(8,128)(2,1)S(1)}, bf16[128,2048]{1,0:T(8,128)(2,1)S(1)}, u32[]{:S(2)}, u32[]{:S(2)}) collective-permute-start(bf16[128,2048]{1,0:T(8,128)(2,1)S(1)} %get-tuple-element.149), channel_id=1, source_target_pairs={{0,1},{4,5},{8,9},{12,13},{16,17},{20,21},{24,25},{28,29}} | collective-permute-start | bytes 1572872 | tf_op jit(solution)/shard_map/ppermute | solution.py:65
  149.8 18.6 %collective-permute-start.15 = (bf16[128,2048]{1,0:T(8,128)(2,1)S(1)}, bf16[128,2048]{1,0:T(8,128)(2,1)S(1)}, u32[]{:S(2)}, u32[]{:S(2)}) collective-permute-start(bf16[128,2048]{1,0:T(8,128)(2,1)S(1)} %get-tuple-element.150), channel_id=1, source_target_pairs={{3,2},{7,6},{11,10},{15,14},{19,18},{23,22},{27,26},{31,30}} | collective-permute-start | bytes 1572872 | tf_op jit(solution)/shard_map/ppermute | solution.py:66
  157.4 22.2 %collective-permute-start.31 = (bf16[128,2048]{1,0:T(8,128)(2,1)S(1)}, bf16[128,2048]{1,0:T(8,128)(2,1)S(1)}, u32[]{:S(2)}, u32[]{:S(2)}) collective-permute-start(bf16[128,2048]{1,0:T(8,128)(2,1)S(1)} %get-tuple-element.153), channel_id=1, source_target_pairs={{0,1},{1,2},{4,5},{5,6},{8,9},{9,10},{12,13},{13,14},{16,17},{17,1... | collective-permute-start | bytes 1572872 | tf_op jit(solution)/shard_map/ppermute | solution.py:65
  161.9 17.8 %collective-permute-start.34 = (bf16[128,2048]{1,0:T(8,128)(2,1)S(1)}, bf16[128,2048]{1,0:T(8,128)(2,1)S(1)}, u32[]{:S(2)}, u32[]{:S(2)}) collective-permute-start(bf16[128,2048]{1,0:T(8,128)(2,1)S(1)} %get-tuple-element.154), channel_id=1, source_target_pairs={{2,1},{3,2},{6,5},{7,6},{10,9},{11,10},{14,13},{15,14},{18,17},{19... | collective-permute-start | bytes 1572872 | tf_op jit(solution)/shard_map/ppermute | solution.py:66
  168.7 22.2 %collective-permute-start.13 = (bf16[128,2048]{1,0:T(8,128)(2,1)S(1)}, bf16[128,2048]{1,0:T(8,128)(2,1)S(1)}, u32[]{:S(2)}, u32[]{:S(2)}) collective-permute-start(bf16[128,2048]{1,0:T(8,128)(2,1)S(1)} %get-tuple-element.147), channel_id=1, source_target_pairs={{0,1},{1,2},{4,5},{5,6},{8,9},{9,10},{12,13},{13,14},{16,17},{17,1... | collective-permute-start | bytes 1572872 | tf_op jit(solution)/shard_map/ppermute | solution.py:65
  173.1 17.8 %collective-permute-start.16 = (bf16[128,2048]{1,0:T(8,128)(2,1)S(1)}, bf16[128,2048]{1,0:T(8,128)(2,1)S(1)}, u32[]{:S(2)}, u32[]{:S(2)}) collective-permute-start(bf16[128,2048]{1,0:T(8,128)(2,1)S(1)} %get-tuple-element.148), channel_id=1, source_target_pairs={{2,1},{3,2},{6,5},{7,6},{10,9},{11,10},{14,13},{15,14},{18,17},{19... | collective-permute-start | bytes 1572872 | tf_op jit(solution)/shard_map/ppermute | solution.py:66
  174.0 23.0 %collective-permute-start.49 = (bf16[128,2048]{1,0:T(8,128)(2,1)S(1)}, bf16[128,2048]{1,0:T(8,128)(2,1)S(1)}, u32[]{:S(2)}, u32[]{:S(2)}) collective-permute-start(bf16[128,2048]{1,0:T(8,128)(2,1)S(1)} %get-tuple-element.167), channel_id=1, source_target_pairs={{1,0},{2,1},{3,2},{5,4},{6,5},{7,6},{9,8},{10,9},{11,10},{13,12},{... | collective-permute-start | bytes 1572872 | tf_op jit(solution)/shard_map/ppermute | solution.py:52
  180.0 25.1 %collective-permute-start.32 = (bf16[128,2048]{1,0:T(8,128)(2,1)S(1)}, bf16[128,2048]{1,0:T(8,128)(2,1)S(1)}, u32[]{:S(2)}, u32[]{:S(2)}) collective-permute-start(bf16[128,2048]{1,0:T(8,128)(2,1)S(1)} %get-tuple-element.151), channel_id=1, source_target_pairs={{0,1},{1,2},{2,3},{4,5},{5,6},{6,7},{8,9},{9,10},{10,11},{12,13},{... | collective-permute-start | bytes 1572872 | tf_op jit(solution)/shard_map/ppermute | solution.py:65
  184.5 22.0 %collective-permute-start.35 = (bf16[128,2048]{1,0:T(8,128)(2,1)S(1)}, bf16[128,2048]{1,0:T(8,128)(2,1)S(1)}, u32[]{:S(2)}, u32[]{:S(2)}) collective-permute-start(bf16[128,2048]{1,0:T(8,128)(2,1)S(1)} %get-tuple-element.152), channel_id=1, source_target_pairs={{1,0},{2,1},{3,2},{5,4},{6,5},{7,6},{9,8},{10,9},{11,10},{13,12},{... | collective-permute-start | bytes 1572872 | tf_op jit(solution)/shard_map/ppermute | solution.py:66
  191.2 22.1 %collective-permute-start.14 = (bf16[128,2048]{1,0:T(8,128)(2,1)S(1)}, bf16[128,2048]{1,0:T(8,128)(2,1)S(1)}, u32[]{:S(2)}, u32[]{:S(2)}) collective-permute-start(bf16[128,2048]{1,0:T(8,128)(2,1)S(1)} %get-tuple-element.145), channel_id=1, source_target_pairs={{0,1},{1,2},{2,3},{4,5},{5,6},{6,7},{8,9},{9,10},{10,11},{12,13},{... | collective-permute-start | bytes 1572872 | tf_op jit(solution)/shard_map/ppermute | solution.py:65
  195.7 17.7 %collective-permute-start.17 = (bf16[128,2048]{1,0:T(8,128)(2,1)S(1)}, bf16[128,2048]{1,0:T(8,128)(2,1)S(1)}, u32[]{:S(2)}, u32[]{:S(2)}) collective-permute-start(bf16[128,2048]{1,0:T(8,128)(2,1)S(1)} %get-tuple-element.146), channel_id=1, source_target_pairs={{1,0},{2,1},{3,2},{5,4},{6,5},{7,6},{9,8},{10,9},{11,10},{13,12},{... | collective-permute-start | bytes 1572872 | tf_op jit(solution)/shard_map/ppermute | solution.py:66
  197.0 22.1 %collective-permute-start.48 = (bf16[128,2048]{1,0:T(8,128)(2,1)S(1)}, bf16[128,2048]{1,0:T(8,128)(2,1)S(1)}, u32[]{:S(2)}, u32[]{:S(2)}) collective-permute-start(bf16[128,2048]{1,0:T(8,128)(2,1)S(1)} %get-tuple-element.167), channel_id=1, source_target_pairs={{0,1},{1,2},{2,3},{4,5},{5,6},{6,7},{8,9},{9,10},{10,11},{12,13},{... | collective-permute-start | bytes 1572872 | tf_op jit(solution)/shard_map/ppermute | solution.py:51
  216.7 21.4 %collective-permute-start.19 = (bf16[128,2048]{1,0:T(8,128)(2,1)S(1)}, bf16[128,2048]{1,0:T(8,128)(2,1)S(1)}, u32[]{:S(2)}, u32[]{:S(2)}) collective-permute-start(bf16[128,2048]{1,0:T(8,128)(2,1)S(1)} %get-tuple-element.72), channel_id=1, source_target_pairs={{1,0},{2,1},{3,2},{5,4},{6,5},{7,6},{9,8},{10,9},{11,10},{13,12},{... | collective-permute-start | bytes 1572872 | tf_op jit(solution)/shard_map/ppermute | solution.py:52
  219.1 20.4 %collective-permute-start.52 = (bf16[128,2048]{1,0:T(8,128)(2,1)S(1)}, bf16[128,2048]{1,0:T(8,128)(2,1)S(1)}, u32[]{:S(2)}, u32[]{:S(2)}) collective-permute-start(bf16[128,2048]{1,0:T(8,128)(2,1)S(1)} %collective-permute-done.48), channel_id=1, source_target_pairs={{1,2},{2,3},{5,6},{6,7},{9,10},{10,11},{13,14},{14,15},{17,18},{18... | collective-permute-start | bytes 1572872 | tf_op jit(solution)/shard_map/ppermute | solution.py:51
  219.8 28.9 %collective-permute-start.51 = (bf16[128,2048]{1,0:T(8,128)(2,1)S(1)}, bf16[128,2048]{1,0:T(8,128)(2,1)S(1)}, u32[]{:S(2)}, u32[]{:S(2)}) collective-permute-start(bf16[128,2048]{1,0:T(8,128)(2,1)S(1)} %collective-permute-done.50), channel_id=1, source_target_pairs={{1,0},{5,4},{9,8},{13,12},{17,16},{21,20},{25,24},{29,28}} | collective-permute-start | bytes 1572872 | tf_op jit(solution)/shard_map/ppermute | solution.py:52
  221.1 28.5 %collective-permute-start.18 = (bf16[128,2048]{1,0:T(8,128)(2,1)S(1)}, bf16[128,2048]{1,0:T(8,128)(2,1)S(1)}, u32[]{:S(2)}, u32[]{:S(2)}) collective-permute-start(bf16[128,2048]{1,0:T(8,128)(2,1)S(1)} %get-tuple-element.72), channel_id=1, source_target_pairs={{0,1},{1,2},{2,3},{4,5},{5,6},{6,7},{8,9},{9,10},{10,11},{12,13},{... | collective-permute-start | bytes 1572872 | tf_op jit(solution)/shard_map/ppermute | solution.py:51
  238.1 17.4 %collective-permute-start.20 = (bf16[128,2048]{1,0:T(8,128)(2,1)S(1)}, bf16[128,2048]{1,0:T(8,128)(2,1)S(1)}, u32[]{:S(2)}, u32[]{:S(2)}) collective-permute-start(bf16[128,2048]{1,0:T(8,128)(2,1)S(1)} %collective-permute-done.19), channel_id=1, source_target_pairs={{1,0},{2,1},{5,4},{6,5},{9,8},{10,9},{13,12},{14,13},{17,16},{18,1... | collective-permute-start | bytes 1572872 | tf_op jit(solution)/shard_map/ppermute | solution.py:52
  239.5 18.3 %collective-permute-start.53 = (bf16[128,2048]{1,0:T(8,128)(2,1)S(1)}, bf16[128,2048]{1,0:T(8,128)(2,1)S(1)}, u32[]{:S(2)}, u32[]{:S(2)}) collective-permute-start(bf16[128,2048]{1,0:T(8,128)(2,1)S(1)} %collective-permute-done.52), channel_id=1, source_target_pairs={{2,3},{6,7},{10,11},{14,15},{18,19},{22,23},{26,27},{30,31}} | collective-permute-start | bytes 1572872 | tf_op jit(solution)/shard_map/ppermute | solution.py:51
  290.9 17.8 %collective-permute-start.24 = (bf16[128,2048]{1,0:T(8,128)(2,1)S(1)}, bf16[128,2048]{1,0:T(8,128)(2,1)S(1)}, u32[]{:S(2)}, u32[]{:S(2)}) collective-permute-start(bf16[128,2048]{1,0:T(8,128)(2,1)S(1)} %get-tuple-element.137), channel_id=1, source_target_pairs={{0,1},{4,5},{8,9},{12,13},{16,17},{20,21},{24,25},{28,29}} | collective-permute-start | bytes 1572872 | tf_op jit(solution)/shard_map/ppermute | solution.py:65
  300.3 26.6 %collective-permute-start.55 = (bf16[128,2048]{1,0:T(8,128)(2,1)S(1)}, bf16[128,2048]{1,0:T(8,128)(2,1)S(1)}, u32[]{:S(2)}, u32[]{:S(2)}) collective-permute-start(bf16[128,2048]{1,0:T(8,128)(2,1)S(1)} %get-tuple-element.129), channel_id=1, source_target_pairs={{0,1},{1,2},{4,5},{5,6},{8,9},{9,10},{12,13},{13,14},{16,17},{17,1... | collective-permute-start | bytes 1572872 | tf_op jit(solution)/shard_map/ppermute | solution.py:65
  304.7 22.2 %collective-permute-start.58 = (bf16[128,2048]{1,0:T(8,128)(2,1)S(1)}, bf16[128,2048]{1,0:T(8,128)(2,1)S(1)}, u32[]{:S(2)}, u32[]{:S(2)}) collective-permute-start(bf16[128,2048]{1,0:T(8,128)(2,1)S(1)} %get-tuple-element.130), channel_id=1, source_target_pairs={{2,1},{3,2},{6,5},{7,6},{10,9},{11,10},{14,13},{15,14},{18,17},{19... | collective-permute-start | bytes 1572872 | tf_op jit(solution)/shard_map/ppermute | solution.py:66
  309.0 31.6 %collective-permute-start.25 = (bf16[128,2048]{1,0:T(8,128)(2,1)S(1)}, bf16[128,2048]{1,0:T(8,128)(2,1)S(1)}, u32[]{:S(2)}, u32[]{:S(2)}) collective-permute-start(bf16[128,2048]{1,0:T(8,128)(2,1)S(1)} %get-tuple-element.135), channel_id=1, source_target_pairs={{0,1},{1,2},{4,5},{5,6},{8,9},{9,10},{12,13},{13,14},{16,17},{17,1... | collective-permute-start | bytes 1572872 | tf_op jit(solution)/shard_map/ppermute | solution.py:65
  327.3 25.5 %collective-permute-start.56 = (bf16[128,2048]{1,0:T(8,128)(2,1)S(1)}, bf16[128,2048]{1,0:T(8,128)(2,1)S(1)}, u32[]{:S(2)}, u32[]{:S(2)}) collective-permute-start(bf16[128,2048]{1,0:T(8,128)(2,1)S(1)} %get-tuple-element.127), channel_id=1, source_target_pairs={{0,1},{1,2},{2,3},{4,5},{5,6},{6,7},{8,9},{9,10},{10,11},{12,13},{... | collective-permute-start | bytes 1572872 | tf_op jit(solution)/shard_map/ppermute | solution.py:65
  351.2 19.5 %collective-permute-start.29 = (bf16[128,2048]{1,0:T(8,128)(2,1)S(1)}, bf16[128,2048]{1,0:T(8,128)(2,1)S(1)}, u32[]{:S(2)}, u32[]{:S(2)}) collective-permute-start(bf16[128,2048]{1,0:T(8,128)(2,1)S(1)} %get-tuple-element.134), channel_id=1, source_target_pairs={{1,0},{2,1},{3,2},{5,4},{6,5},{7,6},{9,8},{10,9},{11,10},{13,12},{... | collective-permute-start | bytes 1572872 | tf_op jit(solution)/shard_map/ppermute | solution.py:66
  376.2 26.6 %collective-permute-start.61 = (bf16[128,2048]{1,0:T(8,128)(2,1)S(1)}, bf16[128,2048]{1,0:T(8,128)(2,1)S(1)}, u32[]{:S(2)}, u32[]{:S(2)}) collective-permute-start(bf16[128,2048]{1,0:T(8,128)(2,1)S(1)} %get-tuple-element.89), channel_id=1, source_target_pairs={{1,0},{2,1},{3,2},{5,4},{6,5},{7,6},{9,8},{10,9},{11,10},{13,12},{... | collective-permute-start | bytes 1572872 | tf_op jit(solution)/shard_map/ppermute | solution.py:52
  377.5 27.3 %collective-permute-start.66 = (bf16[128,2048]{1,0:T(8,128)(2,1)S(1)}, bf16[128,2048]{1,0:T(8,128)(2,1)S(1)}, u32[]{:S(2)}, u32[]{:S(2)}) collective-permute-start(bf16[128,2048]{1,0:T(8,128)(2,1)S(1)} %get-tuple-element.164), channel_id=1, source_target_pairs={{0,1},{1,2},{2,3},{4,5},{5,6},{6,7},{8,9},{9,10},{10,11},{12,13},{... | collective-permute-start | bytes 1572872 | tf_op jit(solution)/shard_map/ppermute | solution.py:51
  382.7 31.3 %collective-permute-start.37 = (bf16[128,2048]{1,0:T(8,128)(2,1)S(1)}, bf16[128,2048]{1,0:T(8,128)(2,1)S(1)}, u32[]{:S(2)}, u32[]{:S(2)}) collective-permute-start(bf16[128,2048]{1,0:T(8,128)(2,1)S(1)} %get-tuple-element.174), channel_id=1, source_target_pairs={{1,0},{2,1},{3,2},{5,4},{6,5},{7,6},{9,8},{10,9},{11,10},{13,12},{... | collective-permute-start | bytes 1572872 | tf_op jit(solution)/shard_map/ppermute | solution.py:52
  384.0 31.3 %collective-permute-start.36 = (bf16[128,2048]{1,0:T(8,128)(2,1)S(1)}, bf16[128,2048]{1,0:T(8,128)(2,1)S(1)}, u32[]{:S(2)}, u32[]{:S(2)}) collective-permute-start(bf16[128,2048]{1,0:T(8,128)(2,1)S(1)} %get-tuple-element.174), channel_id=1, source_target_pairs={{0,1},{1,2},{2,3},{4,5},{5,6},{6,7},{8,9},{9,10},{10,11},{12,13},{... | collective-permute-start | bytes 1572872 | tf_op jit(solution)/shard_map/ppermute | solution.py:51
  391.5 33.7 %collective-permute-start.68 = (bf16[128,2048]{1,0:T(8,128)(2,1)S(1)}, bf16[128,2048]{1,0:T(8,128)(2,1)S(1)}, u32[]{:S(2)}, u32[]{:S(2)}) collective-permute-start(bf16[128,2048]{1,0:T(8,128)(2,1)S(1)} %collective-permute-done.67), channel_id=1, source_target_pairs={{1,0},{2,1},{5,4},{6,5},{9,8},{10,9},{13,12},{14,13},{17,16},{18,1... | collective-permute-start | bytes 1572872 | tf_op jit(solution)/shard_map/ppermute | solution.py:52
  402.8 23.8 %collective-permute-start.60 = (bf16[128,2048]{1,0:T(8,128)(2,1)S(1)}, bf16[128,2048]{1,0:T(8,128)(2,1)S(1)}, u32[]{:S(2)}, u32[]{:S(2)}) collective-permute-start(bf16[128,2048]{1,0:T(8,128)(2,1)S(1)} %get-tuple-element.89), channel_id=1, source_target_pairs={{0,1},{1,2},{2,3},{4,5},{5,6},{6,7},{8,9},{9,10},{10,11},{12,13},{... | collective-permute-start | bytes 1572872 | tf_op jit(solution)/shard_map/ppermute | solution.py:51
  404.8 23.1 %collective-permute-start.70 = (bf16[128,2048]{1,0:T(8,128)(2,1)S(1)}, bf16[128,2048]{1,0:T(8,128)(2,1)S(1)}, u32[]{:S(2)}, u32[]{:S(2)}) collective-permute-start(bf16[128,2048]{1,0:T(8,128)(2,1)S(1)} %collective-permute-done.66), channel_id=1, source_target_pairs={{1,2},{2,3},{5,6},{6,7},{9,10},{10,11},{13,14},{14,15},{17,18},{18... | collective-permute-start | bytes 1572872 | tf_op jit(solution)/shard_map/ppermute | solution.py:51
  414.0 22.2 %collective-permute-start.38 = (bf16[128,2048]{1,0:T(8,128)(2,1)S(1)}, bf16[128,2048]{1,0:T(8,128)(2,1)S(1)}, u32[]{:S(2)}, u32[]{:S(2)}) collective-permute-start(bf16[128,2048]{1,0:T(8,128)(2,1)S(1)} %collective-permute-done.37), channel_id=1, source_target_pairs={{1,0},{2,1},{5,4},{6,5},{9,8},{10,9},{13,12},{14,13},{17,16},{18,1... | collective-permute-start | bytes 1572872 | tf_op jit(solution)/shard_map/ppermute | solution.py:52
  415.3 21.6 %collective-permute-start.40 = (bf16[128,2048]{1,0:T(8,128)(2,1)S(1)}, bf16[128,2048]{1,0:T(8,128)(2,1)S(1)}, u32[]{:S(2)}, u32[]{:S(2)}) collective-permute-start(bf16[128,2048]{1,0:T(8,128)(2,1)S(1)} %collective-permute-done.36), channel_id=1, source_target_pairs={{1,2},{2,3},{5,6},{6,7},{9,10},{10,11},{13,14},{14,15},{17,18},{18... | collective-permute-start | bytes 1572872 | tf_op jit(solution)/shard_map/ppermute | solution.py:51
  426.6 59.2 %collective-permute-start.62 = (bf16[128,2048]{1,0:T(8,128)(2,1)S(1)}, bf16[128,2048]{1,0:T(8,128)(2,1)S(1)}, u32[]{:S(2)}, u32[]{:S(2)}) collective-permute-start(bf16[128,2048]{1,0:T(8,128)(2,1)S(1)} %collective-permute-done.61), channel_id=1, source_target_pairs={{1,0},{2,1},{5,4},{6,5},{9,8},{10,9},{13,12},{14,13},{17,16},{18,1... | collective-permute-start | bytes 1572872 | tf_op jit(solution)/shard_map/ppermute | solution.py:52
  427.9 58.6 %collective-permute-start.64 = (bf16[128,2048]{1,0:T(8,128)(2,1)S(1)}, bf16[128,2048]{1,0:T(8,128)(2,1)S(1)}, u32[]{:S(2)}, u32[]{:S(2)}) collective-permute-start(bf16[128,2048]{1,0:T(8,128)(2,1)S(1)} %collective-permute-done.60), channel_id=1, source_target_pairs={{1,2},{2,3},{5,6},{6,7},{9,10},{10,11},{13,14},{14,15},{17,18},{18... | collective-permute-start | bytes 1572872 | tf_op jit(solution)/shard_map/ppermute | solution.py:51
  436.2 18.7 %collective-permute-start.71 = (bf16[128,2048]{1,0:T(8,128)(2,1)S(1)}, bf16[128,2048]{1,0:T(8,128)(2,1)S(1)}, u32[]{:S(2)}, u32[]{:S(2)}) collective-permute-start(bf16[128,2048]{1,0:T(8,128)(2,1)S(1)} %collective-permute-done.70), channel_id=1, source_target_pairs={{2,3},{6,7},{10,11},{14,15},{18,19},{22,23},{26,27},{30,31}} | collective-permute-start | bytes 1572872 | tf_op jit(solution)/shard_map/ppermute | solution.py:51
  486.5 19.4 %collective-permute-start.63 = (bf16[128,2048]{1,0:T(8,128)(2,1)S(1)}, bf16[128,2048]{1,0:T(8,128)(2,1)S(1)}, u32[]{:S(2)}, u32[]{:S(2)}) collective-permute-start(bf16[128,2048]{1,0:T(8,128)(2,1)S(1)} %collective-permute-done.62), channel_id=1, source_target_pairs={{1,0},{5,4},{9,8},{13,12},{17,16},{21,20},{25,24},{29,28}} | collective-permute-start | bytes 1572872 | tf_op jit(solution)/shard_map/ppermute | solution.py:52
  488.6 39.8 %collective-permute-start.65 = (bf16[128,2048]{1,0:T(8,128)(2,1)S(1)}, bf16[128,2048]{1,0:T(8,128)(2,1)S(1)}, u32[]{:S(2)}, u32[]{:S(2)}) collective-permute-start(bf16[128,2048]{1,0:T(8,128)(2,1)S(1)} %collective-permute-done.64), channel_id=1, source_target_pairs={{2,3},{6,7},{10,11},{14,15},{18,19},{22,23},{26,27},{30,31}} | collective-permute-start | bytes 1572872 | tf_op jit(solution)/shard_map/ppermute | solution.py:51
  490.0 21.1 %collective-permute-start.43 = (bf16[128,2048]{1,0:T(8,128)(2,1)S(1)}, bf16[128,2048]{1,0:T(8,128)(2,1)S(1)}, u32[]{:S(2)}, u32[]{:S(2)}) collective-permute-start(bf16[128,2048]{1,0:T(8,128)(2,1)S(1)} %get-tuple-element.141), channel_id=1, source_target_pairs={{0,1},{1,2},{4,5},{5,6},{8,9},{9,10},{12,13},{13,14},{16,17},{17,1... | collective-permute-start | bytes 1572872 | tf_op jit(solution)/shard_map/ppermute | solution.py:65
  500.8 20.5 %collective-permute-start.73 = (bf16[128,2048]{1,0:T(8,128)(2,1)S(1)}, bf16[128,2048]{1,0:T(8,128)(2,1)S(1)}, u32[]{:S(2)}, u32[]{:S(2)}) collective-permute-start(bf16[128,2048]{1,0:T(8,128)(2,1)S(1)} %get-tuple-element.123), channel_id=1, source_target_pairs={{0,1},{1,2},{4,5},{5,6},{8,9},{9,10},{12,13},{13,14},{16,17},{17,1... | collective-permute-start | bytes 1572872 | tf_op jit(solution)/shard_map/ppermute | solution.py:65
  609.4 202.0 %reduce-scatter.4.cloned.1.call-start = ((), (), s32[]{:S(2)}) async-start(), calls=%async_computation.6 | async-start | bytes 8699904 | tf_op jit(solution)/shard_map/reduce_scatter | solution.py:204
  641.5 194.2 %reduce-scatter.8.cloned.1.call-start = ((), (), s32[]{:S(2)}) async-start(), calls=%async_computation.8 | async-start | bytes 11943936 | tf_op jit(solution)/shard_map/reduce_scatter | solution.py:180
  712.3 22.1 %collective-permute-start.85 = (bf16[128,2048]{1,0:T(8,128)(2,1)S(1)}, bf16[128,2048]{1,0:T(8,128)(2,1)S(1)}, u32[]{:S(2)}, u32[]{:S(2)}) collective-permute-start(bf16[128,2048]{1,0:T(8,128)(2,1)S(1)} %get-tuple-element.111), channel_id=1, source_target_pairs={{0,1},{1,2},{4,5},{5,6},{8,9},{9,10},{12,13},{13,14},{16,17},{17,1... | collective-permute-start | bytes 1572872 | tf_op jit(solution)/shard_map/ppermute | solution.py:65
  716.7 17.6 %collective-permute-start.88 = (bf16[128,2048]{1,0:T(8,128)(2,1)S(1)}, bf16[128,2048]{1,0:T(8,128)(2,1)S(1)}, u32[]{:S(2)}, u32[]{:S(2)}) collective-permute-start(bf16[128,2048]{1,0:T(8,128)(2,1)S(1)} %get-tuple-element.112), channel_id=1, source_target_pairs={{2,1},{3,2},{6,5},{7,6},{10,9},{11,10},{14,13},{15,14},{18,17},{19... | collective-permute-start | bytes 1572872 | tf_op jit(solution)/shard_map/ppermute | solution.py:66
  (149 other events, 2253.3 us)
Sparse Core Ops, SparseCore 0:
  12.0 71.3 all-gather.3
  85.3 34.4 all-gather.5
  121.6 65.7 all-gather.7
  609.5 67.7 reduce-scatter.5
  680.6 68.6 reduce-scatter.3
  752.6 83.0 reduce-scatter.7
where the time goes:
time: 856 us; the launch traced here: 847 us
  waiting for transfers between devices  283 us (33%)
  starting transfers between devices  234 us (27%)
  matrix products  159 us (19%)
  other arithmetic  87.5 us (10%)
  blocking collectives  40.4 us (5%)
  local copies, waits for them, and re-layouts  26.1 us (3%)
  between operations  17.2 us (2%)
    ppermute x24, waiting for transfers between devices, line_gather(): l = lax.ppermute(l, 'mp', [(i, i - 1) for i in range(1, n - step + 1)])  154 us
    ppermute x24, starting transfers between devices, line_scatter(): r = lax.ppermute(send_r, 'mp', [(i, i + 1) for i in range(step)])  113 us
    ppermute x24, waiting for transfers between devices, line_scatter(): r = lax.ppermute(send_r, 'mp', [(i, i + 1) for i in range(step)])  79.5 us
    ppermute x24, starting transfers between devices, line_gather(): r = lax.ppermute(r, 'mp', [(i, i + 1) for i in range(step - 1, n - 1)])  66.8 us
    dot_general x5, matrix products, dot_tn(): lax.dot_general(a, b, (((0,), (0,)), ((), ())), preferred_element_type=F32)  51.7 us
    dot_general x8, matrix products, dot_nt(): lax.dot_general(a, b, (((1,), (1,)), ((), ())), preferred_element_type=F32)  48.2 us
    dot_general x8, matrix products, dot_nn(): lax.dot_general(a, b, (((1,), (0,)), ((), ())), preferred_element_type=F32)  43.3 us
    psum x1, blocking collectives, body(): lax.psum(jnp.stack([sum(first_gain), sum(second_gain)]), ('dp', 'mp'))  40.4 us
  transfers between devices with their start and end apart: 102, of which 44 were waited for; matrix products, arithmetic and copies ran while one was open for 24% of the time, Pallas kernels for 0%

commit v1 on v0

--- a/solution.py
+++ b/solution.py
@@ -210,7 +210,9 @@
         input_gradient.append(
             middle_grad[h] + norm_back(first_grad * first_norm_gain, first_hat[h], first_scale[h])
         )
-    gains = lax.psum(jnp.stack([sum(first_gain), sum(second_gain)]), ("dp", "mp"))
+    gains = jnp.sum(
+        lax.all_gather(jnp.stack([sum(first_gain), sum(second_gain)]), ("dp", "mp")), axis=0
+    )
     return (
         jnp.concatenate(outputs, axis=0).astype(BF),
         jnp.concatenate(input_gradient, axis=0),

time: 856 us -> 872 us (1.019)
  blocking collectives: 40.4 us -> 75.2 us
  waiting for transfers between devices: 283 us -> 263 us
    all_gather x0 -> x1, blocking collectives: none -> 75.2 us  [body(): lax.all_gather(jnp.stack([sum(first_gain), sum(second_gain)]), ('dp', 'mp'))]
    psum x1 -> x0, blocking collectives: 40.4 us -> none  [body(): lax.psum(jnp.stack([sum(first_gain), sum(second_gain)]), ('dp', 'mp'))]
    reduce_scatter x1, waiting for transfers between devices: 19.9 us -> 0.01 us  [body(): lax.psum_scatter(grads_two, 'dp', scatter_dimension=1, tiled=True)]
    unnamed x27 -> x28, other arithmetic: 24.3 us -> 24.3 us
  transfers between devices with their start and end apart: 102 -> 102, of which waited for: 44 -> 43; matrix products, arithmetic and copies ran while one was open for 24% -> 24% of each run, Pallas kernels for 0% -> 0%
where the time goes in v1:
time: 872 us; the launch traced here: 863 us
  waiting for transfers between devices  263 us (30%)
  starting transfers between devices  234 us (27%)
  matrix products  159 us (18%)
  other arithmetic  88.7 us (10%)
  blocking collectives  75.2 us (9%)
  local copies, waits for them, and re-layouts  26.1 us (3%)
  between operations  17.2 us (2%)
    ppermute x24, waiting for transfers between devices, line_gather(): l = lax.ppermute(l, 'mp', [(i, i - 1) for i in range(1, n - step + 1)])  154 us
    ppermute x24, starting transfers between devices, line_scatter(): r = lax.ppermute(send_r, 'mp', [(i, i + 1) for i in range(step)])  113 us
    ppermute x24, waiting for transfers between devices, line_scatter(): r = lax.ppermute(send_r, 'mp', [(i, i + 1) for i in range(step)])  79.5 us
    all_gather x1, blocking collectives, body(): lax.all_gather(jnp.stack([sum(first_gain), sum(second_gain)]), ('dp', 'mp'))  75.2 us
    ppermute x24, starting transfers between devices, line_gather(): r = lax.ppermute(r, 'mp', [(i, i + 1) for i in range(step - 1, n - 1)])  66.8 us
    dot_general x5, matrix products, dot_tn(): lax.dot_general(a, b, (((0,), (0,)), ((), ())), preferred_element_type=F32)  51.7 us
    dot_general x8, matrix products, dot_nt(): lax.dot_general(a, b, (((1,), (1,)), ((), ())), preferred_element_type=F32)  48.2 us
    dot_general x8, matrix products, dot_nn(): lax.dot_general(a, b, (((1,), (0,)), ((), ())), preferred_element_type=F32)  43.3 us
  transfers between devices with their start and end apart: 102, of which 43 were waited for; matrix products, arithmetic and copies ran while one was open for 24% of the time, Pallas kernels for 0%

profile of v1, /device:TPU:0, one launch (start us, length us, event | category | flops | bytes accessed | tf_op | source)
XLA Modules:
  0.0 863.0 jit_solution(12415559917782110727)
XLA Ops:
  15.7 5.6 collective-permute-start
  21.3 10.0 %collective-permute-done.1 = bf16[128,2048]{1,0:T(8,128)(2,1)S(1)} collective-permute-done((bf16[128,2048]{1,0:T(8,128)(2,1)S(1)}, bf16[128,2048]{1,0:T(8,128)(2,1)S(1)}, u32[]{:S(2)}, u32[]{:S(2)}) %collective-permute-start.1) | collective-permute-done | bytes 524320 | tf_op jit(solution)/shard_map/ppermute | solution.py:52
  33.3 13.1 %collective-permute-done.2 = bf16[128,2048]{1,0:T(8,128)(2,1)S(1)} collective-permute-done((bf16[128,2048]{1,0:T(8,128)(2,1)S(1)}, bf16[128,2048]{1,0:T(8,128)(2,1)S(1)}, u32[]{:S(2)}, u32[]{:S(2)}) %collective-permute-start.2) | collective-permute-done | bytes 524320 | tf_op jit(solution)/shard_map/ppermute | solution.py:52
  48.6 12.1 %collective-permute-done.3 = bf16[128,2048]{1,0:T(8,128)(2,1)} collective-permute-done((bf16[128,2048]{1,0:T(8,128)(2,1)S(1)}, bf16[128,2048]{1,0:T(8,128)(2,1)}, u32[]{:S(2)}, u32[]{:S(2)}) %collective-permute-start.3) | collective-permute-done | bytes 524320 | tf_op jit(solution)/shard_map/ppermute | solution.py:52
  73.0 6.1 collective-permute-done.7
  83.5 8.2 collective-permute-done.8
  95.1 8.5 collective-permute-done.9
  107.4 8.1 fusion.74
  132.7 6.0 fusion.27
  150.5 6.6 collective-permute-done.30
  162.6 5.8 collective-permute-done.12
  197.0 8.1 collective-permute-start.48
  206.4 6.9 collective-permute-done.14
  221.1 17.0 %collective-permute-start.18 = (bf16[128,2048]{1,0:T(8,128)(2,1)S(1)}, bf16[128,2048]{1,0:T(8,128)(2,1)S(1)}, u32[]{:S(2)}, u32[]{:S(2)}) collective-permute-start(bf16[128,2048]{1,0:T(8,128)(2,1)S(1)} %get-tuple-element.84), channel_id=1, source_target_pairs={{0,1},{1,2},{2,3},{4,5},{5,6},{6,7},{8,9},{9,10},{10,11},{12,13},{... | collective-permute-start | bytes 1572872 | tf_op jit(solution)/shard_map/ppermute | solution.py:51
  240.2 8.6 collective-permute-done.51
  259.9 7.3 collective-permute-done.21
  270.7 7.8 fusion.6
  293.0 7.0 collective-permute-done.54
  309.0 16.9 %collective-permute-start.25 = (bf16[128,2048]{1,0:T(8,128)(2,1)S(1)}, bf16[128,2048]{1,0:T(8,128)(2,1)S(1)}, u32[]{:S(2)}, u32[]{:S(2)}) collective-permute-start(bf16[128,2048]{1,0:T(8,128)(2,1)S(1)} %get-tuple-element.147), channel_id=1, source_target_pairs={{0,1},{1,2},{4,5},{5,6},{8,9},{9,10},{12,13},{13,14},{16,17},{17,1... | collective-permute-start | bytes 1572872 | tf_op jit(solution)/shard_map/ppermute | solution.py:65
  327.3 12.0 %collective-permute-start.56 = (bf16[128,2048]{1,0:T(8,128)(2,1)S(1)}, bf16[128,2048]{1,0:T(8,128)(2,1)S(1)}, u32[]{:S(2)}, u32[]{:S(2)}) collective-permute-start(bf16[128,2048]{1,0:T(8,128)(2,1)S(1)} %get-tuple-element.139), channel_id=1, source_target_pairs={{0,1},{1,2},{2,3},{4,5},{5,6},{6,7},{8,9},{9,10},{10,11},{12,13},{... | collective-permute-start | bytes 1572872 | tf_op jit(solution)/shard_map/ppermute | solution.py:65
  341.1 10.1 %collective-permute-start.26 = (bf16[128,2048]{1,0:T(8,128)(2,1)S(1)}, bf16[128,2048]{1,0:T(8,128)(2,1)S(1)}, u32[]{:S(2)}, u32[]{:S(2)}) collective-permute-start(bf16[128,2048]{1,0:T(8,128)(2,1)S(1)} %get-tuple-element.145), channel_id=1, source_target_pairs={{0,1},{1,2},{2,3},{4,5},{5,6},{6,7},{8,9},{9,10},{10,11},{12,13},{... | collective-permute-start | bytes 1572872 | tf_op jit(solution)/shard_map/ppermute | solution.py:65
  357.8 12.8 %collective-permute-done.29 = bf16[128,2048]{1,0:T(8,128)(2,1)S(1)} collective-permute-done((bf16[128,2048]{1,0:T(8,128)(2,1)S(1)}, bf16[128,2048]{1,0:T(8,128)(2,1)S(1)}, u32[]{:S(2)}, u32[]{:S(2)}) %collective-permute-start.29) | collective-permute-done | bytes 524320 | tf_op jit(solution)/shard_map/ppermute | solution.py:66
  392.8 9.9 %collective-permute-done.61 = bf16[128,2048]{1,0:T(8,128)(2,1)S(1)} collective-permute-done((bf16[128,2048]{1,0:T(8,128)(2,1)S(1)}, bf16[128,2048]{1,0:T(8,128)(2,1)S(1)}, u32[]{:S(2)}, u32[]{:S(2)}) %collective-permute-start.61) | collective-permute-done | bytes 524320 | tf_op jit(solution)/shard_map/ppermute | solution.py:52
  405.5 8.5 collective-permute-done.37
  416.0 9.2 %collective-permute-done.68 = bf16[128,2048]{1,0:T(8,128)(2,1)S(1)} collective-permute-done((bf16[128,2048]{1,0:T(8,128)(2,1)S(1)}, bf16[128,2048]{1,0:T(8,128)(2,1)S(1)}, u32[]{:S(2)}, u32[]{:S(2)}) %collective-permute-start.68) | collective-permute-done | bytes 524320 | tf_op jit(solution)/shard_map/ppermute | solution.py:52
  428.6 7.7 collective-permute-done.38
  444.4 8.7 %collective-permute-done.39 = bf16[128,2048]{1,0:T(8,128)(2,1)S(1)} collective-permute-done((bf16[128,2048]{1,0:T(8,128)(2,1)S(1)}, bf16[128,2048]{1,0:T(8,128)(2,1)S(1)}, u32[]{:S(2)}, u32[]{:S(2)}) %collective-permute-start.39) | collective-permute-done | bytes 524320 | tf_op jit(solution)/shard_map/ppermute | solution.py:52
  456.8 7.2 fusion.4
  464.0 5.3 fusion.90
  477.0 7.2 fusion.34
  494.4 5.4 collective-permute-done.72
  529.2 6.3 collective-permute-done.74
  535.5 6.1 collective-permute-done.77
  546.8 7.6 collective-permute-start.78
  554.4 6.6 collective-permute-done.79
  563.0 9.1 %collective-permute-done.80 = bf16[128,2048]{1,0:T(8,128)(2,1)S(1)} collective-permute-done((bf16[128,2048]{1,0:T(8,128)(2,1)S(1)}, bf16[128,2048]{1,0:T(8,128)(2,1)S(1)}, u32[]{:S(2)}, u32[]{:S(2)}) %collective-permute-start.80) | collective-permute-done | bytes 524320 | tf_op jit(solution)/shard_map/ppermute | solution.py:52
  574.1 9.1 %collective-permute-done.81 = bf16[128,2048]{1,0:T(8,128)(2,1)S(1)} collective-permute-done((bf16[128,2048]{1,0:T(8,128)(2,1)S(1)}, bf16[128,2048]{1,0:T(8,128)(2,1)S(1)}, u32[]{:S(2)}, u32[]{:S(2)}) %collective-permute-start.81) | collective-permute-done | bytes 524320 | tf_op jit(solution)/shard_map/ppermute | solution.py:52
  588.9 6.6 fusion.159
  602.1 7.3 pad_maximum_fusion.1
  628.1 13.3 %convolution_convert_fusion.1 = bf16[1888,2048]{1,0:T(8,128)(2,1)} fusion(bf16[1024,2048]{1,0:T(8,128)(2,1)S(1)} %copy-done.50, bf16[1024,864]{0,1:T(8,128)(2,1)S(1)} %bitcast.94, bf16[1024,512]{0,1:T(8,128)(2,1)S(1)} %bitcast.102, bf16[1024,512]{0,1:T(8,128)(2,1)S(1)} %bitcast.104), kind=kOutput, calls=%fused_computation.5 | convolution fusion | flops 7934312448 | bytes 15794176 | tf_op jit(solution)/shard_map/dot_general | solution.py:44
  641.8 6.7 convolution_convert_fusion.2
  648.5 21.0 %convolution_convert_fusion = bf16[1728,2048]{1,0:T(8,128)(2,1)S(1)} fusion(bf16[1024,2048]{1,0:T(8,128)(2,1)} %get-tuple-element.69, bf16[512,864]{0,1:T(8,128)(2,1)S(1)} %copy-done.88, bf16[512,864]{0,1:T(8,128)(2,1)S(1)} %copy-done.86, bf16[512,864]{0,1:T(8,128)(2,1)S(1)} %copy-done.84, bf16[512,864]{0,1:T(8,128)(2,1)S(1)} %copy-done.82), kind=kOutput, calls=%fused_computation.4 | convolution fusion | flops 7265452032 | bytes 14811136 | tf_op jit(solution)/shard_map/dot_general | solution.py:44
  669.5 12.8 %pad_maximum_fusion = bf16[2592,2048]{1,0:T(8,128)(2,1)} fusion(bf16[864,2048]{1,0:T(8,128)(2,1)S(1)} %convolution_convert_fusion.2, bf16[1728,2048]{1,0:T(8,128)(2,1)S(1)} %convolution_convert_fusion), kind=kLoop, calls=%fused_computation | loop fusion | flops 21233664 | bytes 21233664 | tf_op jit(solution)/shard_map/concatenate | solution.py:173
  688.1 10.2 %convolution_convert_fusion.6 = bf16[512,2048]{1,0:T(8,128)(2,1)S(1)} fusion(bf16[2752,2048]{1,0:T(8,128)(2,1)} %all-gather.6.cloned.1.call-done, bf16[1024,2752]{0,1:T(8,128)(2,1)S(1)} %pad_maximum_fusion.2), kind=kOutput, calls=%fused_computation.55 | convolution fusion | flops 5772410880 | bytes 16187392 | tf_op jit(solution)/shard_map/dot_general | solution.py:40
  700.5 6.6 convolution_convert_fusion.5
  717.4 5.8 collective-permute-done.90
  740.9 7.9 collective-permute-start.92
  761.2 75.2 %all-gather.1 = f32[32,2,2048]{2,1,0:T(2,128)} all-gather(f32[1,2,2048]{2,1,0:T(2,128)S(1)} %maximum_bitcast_fusion), channel_id=2, replica_groups=mesh['dp'=8,'mp'=4] {'dp','mp'}, dimensions={0}, use_global_device_ids=true | all-gather | bytes 540672 | tf_op jit(solution)/shard_map/all_gather | solution.py:214
  (504 shorter events, 353.7 us)
Async XLA Ops:
  7.2 100.2 %all-gather.6.cloned.1.call-start = ((), (), s32[]{:S(2)}) async-start(), calls=%async_computation.3 | async-start | bytes 12681216 | tf_op jit(solution)/shard_map/all_gather | solution.py:94
  11.9 126.8 %all-gather.8.cloned.1.call-start = ((), (), s32[]{:S(2)}) async-start(), calls=%async_computation.4 | async-start | bytes 3981312 | tf_op jit(solution)/shard_map/all_gather | solution.py:95
  12.6 258.0 %all-gather.10.cloned.1.call-start = ((), (), s32[]{:S(2)}) async-start(), calls=%async_computation.5 | async-start | bytes 11943936 | tf_op jit(solution)/shard_map/all_gather | solution.py:97
  68.2 774.9 %reduce-scatter.6.cloned.1.call-start = ((), (), s32[]{:S(2)}) async-start(), calls=%async_computation.7 | async-start | bytes 7962624 | tf_op jit(solution)/shard_map/reduce_scatter | solution.py:192
  148.4 20.0 %collective-permute-start.12 = (bf16[128,2048]{1,0:T(8,128)(2,1)S(1)}, bf16[128,2048]{1,0:T(8,128)(2,1)S(1)}, u32[]{:S(2)}, u32[]{:S(2)}) collective-permute-start(bf16[128,2048]{1,0:T(8,128)(2,1)S(1)} %get-tuple-element.161), channel_id=1, source_target_pairs={{0,1},{4,5},{8,9},{12,13},{16,17},{20,21},{24,25},{28,29}} | collective-permute-start | bytes 1572872 | tf_op jit(solution)/shard_map/ppermute | solution.py:65
  149.8 18.6 %collective-permute-start.15 = (bf16[128,2048]{1,0:T(8,128)(2,1)S(1)}, bf16[128,2048]{1,0:T(8,128)(2,1)S(1)}, u32[]{:S(2)}, u32[]{:S(2)}) collective-permute-start(bf16[128,2048]{1,0:T(8,128)(2,1)S(1)} %get-tuple-element.162), channel_id=1, source_target_pairs={{3,2},{7,6},{11,10},{15,14},{19,18},{23,22},{27,26},{31,30}} | collective-permute-start | bytes 1572872 | tf_op jit(solution)/shard_map/ppermute | solution.py:66
  157.4 22.2 %collective-permute-start.31 = (bf16[128,2048]{1,0:T(8,128)(2,1)S(1)}, bf16[128,2048]{1,0:T(8,128)(2,1)S(1)}, u32[]{:S(2)}, u32[]{:S(2)}) collective-permute-start(bf16[128,2048]{1,0:T(8,128)(2,1)S(1)} %get-tuple-element.165), channel_id=1, source_target_pairs={{0,1},{1,2},{4,5},{5,6},{8,9},{9,10},{12,13},{13,14},{16,17},{17,1... | collective-permute-start | bytes 1572872 | tf_op jit(solution)/shard_map/ppermute | solution.py:65
  161.9 17.8 %collective-permute-start.34 = (bf16[128,2048]{1,0:T(8,128)(2,1)S(1)}, bf16[128,2048]{1,0:T(8,128)(2,1)S(1)}, u32[]{:S(2)}, u32[]{:S(2)}) collective-permute-start(bf16[128,2048]{1,0:T(8,128)(2,1)S(1)} %get-tuple-element.166), channel_id=1, source_target_pairs={{2,1},{3,2},{6,5},{7,6},{10,9},{11,10},{14,13},{15,14},{18,17},{19... | collective-permute-start | bytes 1572872 | tf_op jit(solution)/shard_map/ppermute | solution.py:66
  168.7 22.2 %collective-permute-start.13 = (bf16[128,2048]{1,0:T(8,128)(2,1)S(1)}, bf16[128,2048]{1,0:T(8,128)(2,1)S(1)}, u32[]{:S(2)}, u32[]{:S(2)}) collective-permute-start(bf16[128,2048]{1,0:T(8,128)(2,1)S(1)} %get-tuple-element.159), channel_id=1, source_target_pairs={{0,1},{1,2},{4,5},{5,6},{8,9},{9,10},{12,13},{13,14},{16,17},{17,1... | collective-permute-start | bytes 1572872 | tf_op jit(solution)/shard_map/ppermute | solution.py:65
  173.1 17.8 %collective-permute-start.16 = (bf16[128,2048]{1,0:T(8,128)(2,1)S(1)}, bf16[128,2048]{1,0:T(8,128)(2,1)S(1)}, u32[]{:S(2)}, u32[]{:S(2)}) collective-permute-start(bf16[128,2048]{1,0:T(8,128)(2,1)S(1)} %get-tuple-element.160), channel_id=1, source_target_pairs={{2,1},{3,2},{6,5},{7,6},{10,9},{11,10},{14,13},{15,14},{18,17},{19... | collective-permute-start | bytes 1572872 | tf_op jit(solution)/shard_map/ppermute | solution.py:66
  174.0 23.0 %collective-permute-start.49 = (bf16[128,2048]{1,0:T(8,128)(2,1)S(1)}, bf16[128,2048]{1,0:T(8,128)(2,1)S(1)}, u32[]{:S(2)}, u32[]{:S(2)}) collective-permute-start(bf16[128,2048]{1,0:T(8,128)(2,1)S(1)} %get-tuple-element.179), channel_id=1, source_target_pairs={{1,0},{2,1},{3,2},{5,4},{6,5},{7,6},{9,8},{10,9},{11,10},{13,12},{... | collective-permute-start | bytes 1572872 | tf_op jit(solution)/shard_map/ppermute | solution.py:52
  180.0 25.1 %collective-permute-start.32 = (bf16[128,2048]{1,0:T(8,128)(2,1)S(1)}, bf16[128,2048]{1,0:T(8,128)(2,1)S(1)}, u32[]{:S(2)}, u32[]{:S(2)}) collective-permute-start(bf16[128,2048]{1,0:T(8,128)(2,1)S(1)} %get-tuple-element.163), channel_id=1, source_target_pairs={{0,1},{1,2},{2,3},{4,5},{5,6},{6,7},{8,9},{9,10},{10,11},{12,13},{... | collective-permute-start | bytes 1572872 | tf_op jit(solution)/shard_map/ppermute | solution.py:65
  184.5 22.0 %collective-permute-start.35 = (bf16[128,2048]{1,0:T(8,128)(2,1)S(1)}, bf16[128,2048]{1,0:T(8,128)(2,1)S(1)}, u32[]{:S(2)}, u32[]{:S(2)}) collective-permute-start(bf16[128,2048]{1,0:T(8,128)(2,1)S(1)} %get-tuple-element.164), channel_id=1, source_target_pairs={{1,0},{2,1},{3,2},{5,4},{6,5},{7,6},{9,8},{10,9},{11,10},{13,12},{... | collective-permute-start | bytes 1572872 | tf_op jit(solution)/shard_map/ppermute | solution.py:66
  191.2 22.1 %collective-permute-start.14 = (bf16[128,2048]{1,0:T(8,128)(2,1)S(1)}, bf16[128,2048]{1,0:T(8,128)(2,1)S(1)}, u32[]{:S(2)}, u32[]{:S(2)}) collective-permute-start(bf16[128,2048]{1,0:T(8,128)(2,1)S(1)} %get-tuple-element.157), channel_id=1, source_target_pairs={{0,1},{1,2},{2,3},{4,5},{5,6},{6,7},{8,9},{9,10},{10,11},{12,13},{... | collective-permute-start | bytes 1572872 | tf_op jit(solution)/shard_map/ppermute | solution.py:65
  195.7 17.7 %collective-permute-start.17 = (bf16[128,2048]{1,0:T(8,128)(2,1)S(1)}, bf16[128,2048]{1,0:T(8,128)(2,1)S(1)}, u32[]{:S(2)}, u32[]{:S(2)}) collective-permute-start(bf16[128,2048]{1,0:T(8,128)(2,1)S(1)} %get-tuple-element.158), channel_id=1, source_target_pairs={{1,0},{2,1},{3,2},{5,4},{6,5},{7,6},{9,8},{10,9},{11,10},{13,12},{... | collective-permute-start | bytes 1572872 | tf_op jit(solution)/shard_map/ppermute | solution.py:66
  197.0 22.1 %collective-permute-start.48 = (bf16[128,2048]{1,0:T(8,128)(2,1)S(1)}, bf16[128,2048]{1,0:T(8,128)(2,1)S(1)}, u32[]{:S(2)}, u32[]{:S(2)}) collective-permute-start(bf16[128,2048]{1,0:T(8,128)(2,1)S(1)} %get-tuple-element.179), channel_id=1, source_target_pairs={{0,1},{1,2},{2,3},{4,5},{5,6},{6,7},{8,9},{9,10},{10,11},{12,13},{... | collective-permute-start | bytes 1572872 | tf_op jit(solution)/shard_map/ppermute | solution.py:51
  216.7 21.4 %collective-permute-start.19 = (bf16[128,2048]{1,0:T(8,128)(2,1)S(1)}, bf16[128,2048]{1,0:T(8,128)(2,1)S(1)}, u32[]{:S(2)}, u32[]{:S(2)}) collective-permute-start(bf16[128,2048]{1,0:T(8,128)(2,1)S(1)} %get-tuple-element.84), channel_id=1, source_target_pairs={{1,0},{2,1},{3,2},{5,4},{6,5},{7,6},{9,8},{10,9},{11,10},{13,12},{... | collective-permute-start | bytes 1572872 | tf_op jit(solution)/shard_map/ppermute | solution.py:52
  219.1 20.4 %collective-permute-start.52 = (bf16[128,2048]{1,0:T(8,128)(2,1)S(1)}, bf16[128,2048]{1,0:T(8,128)(2,1)S(1)}, u32[]{:S(2)}, u32[]{:S(2)}) collective-permute-start(bf16[128,2048]{1,0:T(8,128)(2,1)S(1)} %collective-permute-done.48), channel_id=1, source_target_pairs={{1,2},{2,3},{5,6},{6,7},{9,10},{10,11},{13,14},{14,15},{17,18},{18... | collective-permute-start | bytes 1572872 | tf_op jit(solution)/shard_map/ppermute | solution.py:51
  219.8 28.9 %collective-permute-start.51 = (bf16[128,2048]{1,0:T(8,128)(2,1)S(1)}, bf16[128,2048]{1,0:T(8,128)(2,1)S(1)}, u32[]{:S(2)}, u32[]{:S(2)}) collective-permute-start(bf16[128,2048]{1,0:T(8,128)(2,1)S(1)} %collective-permute-done.50), channel_id=1, source_target_pairs={{1,0},{5,4},{9,8},{13,12},{17,16},{21,20},{25,24},{29,28}} | collective-permute-start | bytes 1572872 | tf_op jit(solution)/shard_map/ppermute | solution.py:52
  221.1 28.5 %collective-permute-start.18 = (bf16[128,2048]{1,0:T(8,128)(2,1)S(1)}, bf16[128,2048]{1,0:T(8,128)(2,1)S(1)}, u32[]{:S(2)}, u32[]{:S(2)}) collective-permute-start(bf16[128,2048]{1,0:T(8,128)(2,1)S(1)} %get-tuple-element.84), channel_id=1, source_target_pairs={{0,1},{1,2},{2,3},{4,5},{5,6},{6,7},{8,9},{9,10},{10,11},{12,13},{... | collective-permute-start | bytes 1572872 | tf_op jit(solution)/shard_map/ppermute | solution.py:51
  238.1 17.4 %collective-permute-start.20 = (bf16[128,2048]{1,0:T(8,128)(2,1)S(1)}, bf16[128,2048]{1,0:T(8,128)(2,1)S(1)}, u32[]{:S(2)}, u32[]{:S(2)}) collective-permute-start(bf16[128,2048]{1,0:T(8,128)(2,1)S(1)} %collective-permute-done.19), channel_id=1, source_target_pairs={{1,0},{2,1},{5,4},{6,5},{9,8},{10,9},{13,12},{14,13},{17,16},{18,1... | collective-permute-start | bytes 1572872 | tf_op jit(solution)/shard_map/ppermute | solution.py:52
  239.5 18.3 %collective-permute-start.53 = (bf16[128,2048]{1,0:T(8,128)(2,1)S(1)}, bf16[128,2048]{1,0:T(8,128)(2,1)S(1)}, u32[]{:S(2)}, u32[]{:S(2)}) collective-permute-start(bf16[128,2048]{1,0:T(8,128)(2,1)S(1)} %collective-permute-done.52), channel_id=1, source_target_pairs={{2,3},{6,7},{10,11},{14,15},{18,19},{22,23},{26,27},{30,31}} | collective-permute-start | bytes 1572872 | tf_op jit(solution)/shard_map/ppermute | solution.py:51
  290.9 17.8 %collective-permute-start.24 = (bf16[128,2048]{1,0:T(8,128)(2,1)S(1)}, bf16[128,2048]{1,0:T(8,128)(2,1)S(1)}, u32[]{:S(2)}, u32[]{:S(2)}) collective-permute-start(bf16[128,2048]{1,0:T(8,128)(2,1)S(1)} %get-tuple-element.149), channel_id=1, source_target_pairs={{0,1},{4,5},{8,9},{12,13},{16,17},{20,21},{24,25},{28,29}} | collective-permute-start | bytes 1572872 | tf_op jit(solution)/shard_map/ppermute | solution.py:65
  300.3 26.6 %collective-permute-start.55 = (bf16[128,2048]{1,0:T(8,128)(2,1)S(1)}, bf16[128,2048]{1,0:T(8,128)(2,1)S(1)}, u32[]{:S(2)}, u32[]{:S(2)}) collective-permute-start(bf16[128,2048]{1,0:T(8,128)(2,1)S(1)} %get-tuple-element.141), channel_id=1, source_target_pairs={{0,1},{1,2},{4,5},{5,6},{8,9},{9,10},{12,13},{13,14},{16,17},{17,1... | collective-permute-start | bytes 1572872 | tf_op jit(solution)/shard_map/ppermute | solution.py:65
  304.7 22.2 %collective-permute-start.58 = (bf16[128,2048]{1,0:T(8,128)(2,1)S(1)}, bf16[128,2048]{1,0:T(8,128)(2,1)S(1)}, u32[]{:S(2)}, u32[]{:S(2)}) collective-permute-start(bf16[128,2048]{1,0:T(8,128)(2,1)S(1)} %get-tuple-element.142), channel_id=1, source_target_pairs={{2,1},{3,2},{6,5},{7,6},{10,9},{11,10},{14,13},{15,14},{18,17},{19... | collective-permute-start | bytes 1572872 | tf_op jit(solution)/shard_map/ppermute | solution.py:66
  309.0 31.6 %collective-permute-start.25 = (bf16[128,2048]{1,0:T(8,128)(2,1)S(1)}, bf16[128,2048]{1,0:T(8,128)(2,1)S(1)}, u32[]{:S(2)}, u32[]{:S(2)}) collective-permute-start(bf16[128,2048]{1,0:T(8,128)(2,1)S(1)} %get-tuple-element.147), channel_id=1, source_target_pairs={{0,1},{1,2},{4,5},{5,6},{8,9},{9,10},{12,13},{13,14},{16,17},{17,1... | collective-permute-start | bytes 1572872 | tf_op jit(solution)/shard_map/ppermute | solution.py:65
  327.3 25.5 %collective-permute-start.56 = (bf16[128,2048]{1,0:T(8,128)(2,1)S(1)}, bf16[128,2048]{1,0:T(8,128)(2,1)S(1)}, u32[]{:S(2)}, u32[]{:S(2)}) collective-permute-start(bf16[128,2048]{1,0:T(8,128)(2,1)S(1)} %get-tuple-element.139), channel_id=1, source_target_pairs={{0,1},{1,2},{2,3},{4,5},{5,6},{6,7},{8,9},{9,10},{10,11},{12,13},{... | collective-permute-start | bytes 1572872 | tf_op jit(solution)/shard_map/ppermute | solution.py:65
  351.2 19.5 %collective-permute-start.29 = (bf16[128,2048]{1,0:T(8,128)(2,1)S(1)}, bf16[128,2048]{1,0:T(8,128)(2,1)S(1)}, u32[]{:S(2)}, u32[]{:S(2)}) collective-permute-start(bf16[128,2048]{1,0:T(8,128)(2,1)S(1)} %get-tuple-element.146), channel_id=1, source_target_pairs={{1,0},{2,1},{3,2},{5,4},{6,5},{7,6},{9,8},{10,9},{11,10},{13,12},{... | collective-permute-start | bytes 1572872 | tf_op jit(solution)/shard_map/ppermute | solution.py:66
  376.2 26.6 %collective-permute-start.61 = (bf16[128,2048]{1,0:T(8,128)(2,1)S(1)}, bf16[128,2048]{1,0:T(8,128)(2,1)S(1)}, u32[]{:S(2)}, u32[]{:S(2)}) collective-permute-start(bf16[128,2048]{1,0:T(8,128)(2,1)S(1)} %get-tuple-element.101), channel_id=1, source_target_pairs={{1,0},{2,1},{3,2},{5,4},{6,5},{7,6},{9,8},{10,9},{11,10},{13,12},{... | collective-permute-start | bytes 1572872 | tf_op jit(solution)/shard_map/ppermute | solution.py:52
  377.5 27.3 %collective-permute-start.66 = (bf16[128,2048]{1,0:T(8,128)(2,1)S(1)}, bf16[128,2048]{1,0:T(8,128)(2,1)S(1)}, u32[]{:S(2)}, u32[]{:S(2)}) collective-permute-start(bf16[128,2048]{1,0:T(8,128)(2,1)S(1)} %get-tuple-element.176), channel_id=1, source_target_pairs={{0,1},{1,2},{2,3},{4,5},{5,6},{6,7},{8,9},{9,10},{10,11},{12,13},{... | collective-permute-start | bytes 1572872 | tf_op jit(solution)/shard_map/ppermute | solution.py:51
  382.7 31.3 %collective-permute-start.37 = (bf16[128,2048]{1,0:T(8,128)(2,1)S(1)}, bf16[128,2048]{1,0:T(8,128)(2,1)S(1)}, u32[]{:S(2)}, u32[]{:S(2)}) collective-permute-start(bf16[128,2048]{1,0:T(8,128)(2,1)S(1)} %get-tuple-element.186), channel_id=1, source_target_pairs={{1,0},{2,1},{3,2},{5,4},{6,5},{7,6},{9,8},{10,9},{11,10},{13,12},{... | collective-permute-start | bytes 1572872 | tf_op jit(solution)/shard_map/ppermute | solution.py:52
  384.0 31.3 %collective-permute-start.36 = (bf16[128,2048]{1,0:T(8,128)(2,1)S(1)}, bf16[128,2048]{1,0:T(8,128)(2,1)S(1)}, u32[]{:S(2)}, u32[]{:S(2)}) collective-permute-start(bf16[128,2048]{1,0:T(8,128)(2,1)S(1)} %get-tuple-element.186), channel_id=1, source_target_pairs={{0,1},{1,2},{2,3},{4,5},{5,6},{6,7},{8,9},{9,10},{10,11},{12,13},{... | collective-permute-start | bytes 1572872 | tf_op jit(solution)/shard_map/ppermute | solution.py:51
  391.5 33.7 %collective-permute-start.68 = (bf16[128,2048]{1,0:T(8,128)(2,1)S(1)}, bf16[128,2048]{1,0:T(8,128)(2,1)S(1)}, u32[]{:S(2)}, u32[]{:S(2)}) collective-permute-start(bf16[128,2048]{1,0:T(8,128)(2,1)S(1)} %collective-permute-done.67), channel_id=1, source_target_pairs={{1,0},{2,1},{5,4},{6,5},{9,8},{10,9},{13,12},{14,13},{17,16},{18,1... | collective-permute-start | bytes 1572872 | tf_op jit(solution)/shard_map/ppermute | solution.py:52
  402.8 23.8 %collective-permute-start.60 = (bf16[128,2048]{1,0:T(8,128)(2,1)S(1)}, bf16[128,2048]{1,0:T(8,128)(2,1)S(1)}, u32[]{:S(2)}, u32[]{:S(2)}) collective-permute-start(bf16[128,2048]{1,0:T(8,128)(2,1)S(1)} %get-tuple-element.101), channel_id=1, source_target_pairs={{0,1},{1,2},{2,3},{4,5},{5,6},{6,7},{8,9},{9,10},{10,11},{12,13},{... | collective-permute-start | bytes 1572872 | tf_op jit(solution)/shard_map/ppermute | solution.py:51
  404.8 23.1 %collective-permute-start.70 = (bf16[128,2048]{1,0:T(8,128)(2,1)S(1)}, bf16[128,2048]{1,0:T(8,128)(2,1)S(1)}, u32[]{:S(2)}, u32[]{:S(2)}) collective-permute-start(bf16[128,2048]{1,0:T(8,128)(2,1)S(1)} %collective-permute-done.66), channel_id=1, source_target_pairs={{1,2},{2,3},{5,6},{6,7},{9,10},{10,11},{13,14},{14,15},{17,18},{18... | collective-permute-start | bytes 1572872 | tf_op jit(solution)/shard_map/ppermute | solution.py:51
  414.0 22.2 %collective-permute-start.38 = (bf16[128,2048]{1,0:T(8,128)(2,1)S(1)}, bf16[128,2048]{1,0:T(8,128)(2,1)S(1)}, u32[]{:S(2)}, u32[]{:S(2)}) collective-permute-start(bf16[128,2048]{1,0:T(8,128)(2,1)S(1)} %collective-permute-done.37), channel_id=1, source_target_pairs={{1,0},{2,1},{5,4},{6,5},{9,8},{10,9},{13,12},{14,13},{17,16},{18,1... | collective-permute-start | bytes 1572872 | tf_op jit(solution)/shard_map/ppermute | solution.py:52
  415.3 21.6 %collective-permute-start.40 = (bf16[128,2048]{1,0:T(8,128)(2,1)S(1)}, bf16[128,2048]{1,0:T(8,128)(2,1)S(1)}, u32[]{:S(2)}, u32[]{:S(2)}) collective-permute-start(bf16[128,2048]{1,0:T(8,128)(2,1)S(1)} %collective-permute-done.36), channel_id=1, source_target_pairs={{1,2},{2,3},{5,6},{6,7},{9,10},{10,11},{13,14},{14,15},{17,18},{18... | collective-permute-start | bytes 1572872 | tf_op jit(solution)/shard_map/ppermute | solution.py:51
  426.6 59.2 %collective-permute-start.62 = (bf16[128,2048]{1,0:T(8,128)(2,1)S(1)}, bf16[128,2048]{1,0:T(8,128)(2,1)S(1)}, u32[]{:S(2)}, u32[]{:S(2)}) collective-permute-start(bf16[128,2048]{1,0:T(8,128)(2,1)S(1)} %collective-permute-done.61), channel_id=1, source_target_pairs={{1,0},{2,1},{5,4},{6,5},{9,8},{10,9},{13,12},{14,13},{17,16},{18,1... | collective-permute-start | bytes 1572872 | tf_op jit(solution)/shard_map/ppermute | solution.py:52
  427.9 58.6 %collective-permute-start.64 = (bf16[128,2048]{1,0:T(8,128)(2,1)S(1)}, bf16[128,2048]{1,0:T(8,128)(2,1)S(1)}, u32[]{:S(2)}, u32[]{:S(2)}) collective-permute-start(bf16[128,2048]{1,0:T(8,128)(2,1)S(1)} %collective-permute-done.60), channel_id=1, source_target_pairs={{1,2},{2,3},{5,6},{6,7},{9,10},{10,11},{13,14},{14,15},{17,18},{18... | collective-permute-start | bytes 1572872 | tf_op jit(solution)/shard_map/ppermute | solution.py:51
  436.2 18.7 %collective-permute-start.71 = (bf16[128,2048]{1,0:T(8,128)(2,1)S(1)}, bf16[128,2048]{1,0:T(8,128)(2,1)S(1)}, u32[]{:S(2)}, u32[]{:S(2)}) collective-permute-start(bf16[128,2048]{1,0:T(8,128)(2,1)S(1)} %collective-permute-done.70), channel_id=1, source_target_pairs={{2,3},{6,7},{10,11},{14,15},{18,19},{22,23},{26,27},{30,31}} | collective-permute-start | bytes 1572872 | tf_op jit(solution)/shard_map/ppermute | solution.py:51
  486.5 19.4 %collective-permute-start.63 = (bf16[128,2048]{1,0:T(8,128)(2,1)S(1)}, bf16[128,2048]{1,0:T(8,128)(2,1)S(1)}, u32[]{:S(2)}, u32[]{:S(2)}) collective-permute-start(bf16[128,2048]{1,0:T(8,128)(2,1)S(1)} %collective-permute-done.62), channel_id=1, source_target_pairs={{1,0},{5,4},{9,8},{13,12},{17,16},{21,20},{25,24},{29,28}} | collective-permute-start | bytes 1572872 | tf_op jit(solution)/shard_map/ppermute | solution.py:52
  488.6 39.8 %collective-permute-start.65 = (bf16[128,2048]{1,0:T(8,128)(2,1)S(1)}, bf16[128,2048]{1,0:T(8,128)(2,1)S(1)}, u32[]{:S(2)}, u32[]{:S(2)}) collective-permute-start(bf16[128,2048]{1,0:T(8,128)(2,1)S(1)} %collective-permute-done.64), channel_id=1, source_target_pairs={{2,3},{6,7},{10,11},{14,15},{18,19},{22,23},{26,27},{30,31}} | collective-permute-start | bytes 1572872 | tf_op jit(solution)/shard_map/ppermute | solution.py:51
  490.0 21.1 %collective-permute-start.43 = (bf16[128,2048]{1,0:T(8,128)(2,1)S(1)}, bf16[128,2048]{1,0:T(8,128)(2,1)S(1)}, u32[]{:S(2)}, u32[]{:S(2)}) collective-permute-start(bf16[128,2048]{1,0:T(8,128)(2,1)S(1)} %get-tuple-element.153), channel_id=1, source_target_pairs={{0,1},{1,2},{4,5},{5,6},{8,9},{9,10},{12,13},{13,14},{16,17},{17,1... | collective-permute-start | bytes 1572872 | tf_op jit(solution)/shard_map/ppermute | solution.py:65
  500.8 20.5 %collective-permute-start.73 = (bf16[128,2048]{1,0:T(8,128)(2,1)S(1)}, bf16[128,2048]{1,0:T(8,128)(2,1)S(1)}, u32[]{:S(2)}, u32[]{:S(2)}) collective-permute-start(bf16[128,2048]{1,0:T(8,128)(2,1)S(1)} %get-tuple-element.135), channel_id=1, source_target_pairs={{0,1},{1,2},{4,5},{5,6},{8,9},{9,10},{12,13},{13,14},{16,17},{17,1... | collective-permute-start | bytes 1572872 | tf_op jit(solution)/shard_map/ppermute | solution.py:65
  609.4 238.1 %reduce-scatter.4.cloned.1.call-start = ((), (), s32[]{:S(2)}) async-start(), calls=%async_computation.6 | async-start | bytes 8699904 | tf_op jit(solution)/shard_map/reduce_scatter | solution.py:204
  641.5 210.3 %reduce-scatter.8.cloned.1.call-start = ((), (), s32[]{:S(2)}) async-start(), calls=%async_computation.8 | async-start | bytes 11943936 | tf_op jit(solution)/shard_map/reduce_scatter | solution.py:180
  712.3 22.1 %collective-permute-start.85 = (bf16[128,2048]{1,0:T(8,128)(2,1)S(1)}, bf16[128,2048]{1,0:T(8,128)(2,1)S(1)}, u32[]{:S(2)}, u32[]{:S(2)}) collective-permute-start(bf16[128,2048]{1,0:T(8,128)(2,1)S(1)} %get-tuple-element.123), channel_id=1, source_target_pairs={{0,1},{1,2},{4,5},{5,6},{8,9},{9,10},{12,13},{13,14},{16,17},{17,1... | collective-permute-start | bytes 1572872 | tf_op jit(solution)/shard_map/ppermute | solution.py:65
  716.7 17.6 %collective-permute-start.88 = (bf16[128,2048]{1,0:T(8,128)(2,1)S(1)}, bf16[128,2048]{1,0:T(8,128)(2,1)S(1)}, u32[]{:S(2)}, u32[]{:S(2)}) collective-permute-start(bf16[128,2048]{1,0:T(8,128)(2,1)S(1)} %get-tuple-element.124), channel_id=1, source_target_pairs={{2,1},{3,2},{6,5},{7,6},{10,9},{11,10},{14,13},{15,14},{18,17},{19... | collective-permute-start | bytes 1572872 | tf_op jit(solution)/shard_map/ppermute | solution.py:66
  (149 other events, 2253.3 us)
Sparse Core Ops, SparseCore 0:
  12.0 71.3 all-gather.5
  85.3 34.4 all-gather.7
  121.6 65.7 all-gather.9
  609.5 67.7 reduce-scatter.5
  680.6 68.6 reduce-scatter.3
  752.6 84.0 reduce-scatter.7
